TPU v7x, 32 devices: a whole 2x2x4 slice. The times are simulated.
32 devices in a mesh: layer: 4 (over z), row: 2 (over core), col: 4 (over y, x).
Axes of the slice: x: 2, y: 2, z: 4, core: 2. Of those that a mesh axis runs over, the one named last changes fastest.
Arguments:
- panels: float32 [4096, 8192], P('row', ('layer', 'col')), may hold values from -0.0625 to 0.0625
- eigvecs: float32 [8192, 2048], P(('layer', 'row'), 'col'), may hold values from -6 to 6
Outputs:
- result: float32 [4096, 2048], P('row', 'col')
All inputs are finite; a program needn't handle non-finite values.
Results may differ from a plain program's by a relative error of at most 0.0001.
Values sent between devices are 32-bit elements; how exact they have to be, the bound alone decides.
No kernel may reach another device: no remote copies, remote signals or barrier semaphores. Data moves between devices by JAX's collectives and lax.ppermute only.
A program may use at most 64 MiB of HBM per device.

v0:
```python
import jax
import jax.numpy as jnp
from jax import lax
from jax.sharding import PartitionSpec as P


def local(panels, eigvecs):
    layer_vecs = lax.all_gather(eigvecs, "row", axis=0, tiled=True)
    partial_sum = jnp.dot(
        lax.all_gather(panels, "col", axis=1, tiled=True),
        layer_vecs,
        preferred_element_type=jnp.float32,
        precision=lax.Precision.HIGHEST,
    )
    result = lax.psum(partial_sum, "layer")
    return result


def solution(mesh):
    in_specs = (P("row", ("layer", "col")), P(("layer", "row"), "col"))
    out_specs = P("row", "col")
    return jax.shard_map(local, mesh=mesh, in_specs=in_specs, out_specs=out_specs, check_vma=False)
```

profile of v0, /device:TPU:0, one launch (start us, length us, event | category | flops | bytes accessed | tf_op | source)
XLA Modules:
  0.0 383.9 jit_solution(4425001586556484213)
XLA Ops:
  6.5 0.0 all-gather.5.cloned.1.call-start
  6.5 0.7 all-gather.5.cloned.1.call-update
  7.3 0.0 all-gather.3.cloned.1.call-start
  7.3 0.7 all-gather.3.cloned.1.call-update
  8.0 0.0 all-reduce.2.cloned.1.call-start
  8.1 17.2 %all-gather.5.cloned.1.call-done = f32[2048,512]{1,0:T(8,128)} async-done(((f32[1024,512]{1,0:T(8,128)}), f32[2048,512]{1,0:T(8,128)}) %all-gather.5.cloned.1.call-update) | async-done | bytes 4194320 | tf_op jit(solution)/shard_map/all_gather | solution.py:8
  25.3 160.3 %all-gather.3.cloned.1.call-done = f32[2048,2048]{1,0:T(8,128)} async-done(((f32[2048,512]{1,0:T(8,128)}), f32[2048,2048]{1,0:T(8,128)}) %all-gather.3.cloned.1.call-update) | async-done | bytes 16777232 | tf_op jit(solution)/shard_map/all_gather | solution.py:10
  185.6 31.9 %fusion = f32[2048,512]{1,0:T(8,128)} fusion(f32[2048,2048]{1,0:T(8,128)} %all-gather.3.cloned.1.call-done, f32[2048,512]{1,0:T(8,128)} %all-gather.5.cloned.1.call-done), kind=kOutput, calls=%fused_computation | convolution fusion | flops 25769803776 | bytes 25165824 | tf_op jit(solution)/shard_map/dot_general | solution.py:9
  217.6 0.0 all-reduce.2.cloned.1.call-update
  217.6 155.1 %all-reduce.2.cloned.1.call-done = f32[2048,512]{1,0:T(8,128)} async-done(((f32[2048,512]{1,0:T(8,128)}), f32[2048,512]{1,0:T(8,128)}) %all-reduce.2.cloned.1.call-update) | async-done | bytes 4194320 | tf_op jit(solution)/shard_map/psum | solution.py:15
  372.7 4.6 %copy.4 = f32[2048,512]{1,0:T(8,128)} copy(f32[2048,512]{1,0:T(8,128)} %all-reduce.2.cloned.1.call-done) | data formatting | bytes 8388608
Async XLA Ops:
  6.5 18.8 %all-gather.5.cloned.1.call-start = ((), (), s32[]{:S(2)}) async-start(), calls=%async_computation.1 | async-start | bytes 6291456 | tf_op jit(solution)/shard_map/all_gather | solution.py:8
  7.3 178.4 %all-gather.3.cloned.1.call-start = ((), (), s32[]{:S(2)}) async-start(), calls=%async_computation | async-start | bytes 20971520 | tf_op jit(solution)/shard_map/all_gather | solution.py:10
  8.0 364.7 %all-reduce.2.cloned.1.call-start = ((), (), s32[]{:S(2)}) async-start(), calls=%async_computation.2 | async-start | bytes 8388608 | tf_op jit(solution)/shard_map/psum | solution.py:15
Sparse Core Ops, SparseCore 0:
  8.9 16.3 all-gather.4
  27.1 158.4 all-gather.2
  217.7 154.9 all-reduce.1
where the time goes:
time: 384 us
  waiting for transfers between devices  334 us (87%)
  matrix products  31.9 us (8%)
  between operations  13.1 us (3%)
  local copies, waits for them, and re-layouts  4.64 us (1%)
    all_gather x1, waiting for transfers between devices, local(): lax.all_gather(panels, 'col', axis=1, tiled=True)  160 us
    psum x1, waiting for transfers between devices, local(): result = lax.psum(partial_sum, 'layer')  155 us
    dot_general x1, matrix products, local(): jnp.dot(lax.all_gather(panels, 'col', axis=1, tiled=True), layer_vecs, pr...  31.9 us
    all_gather x1, waiting for transfers between devices, local(): layer_vecs = lax.all_gather(eigvecs, 'row', axis=0, tiled=True)  17.2 us
  transfers between devices with their start and end apart: 3, of which 3 were waited for; matrix products, arithmetic and copies ran while one was open for 0% of the time, Pallas kernels for 0%

commit v1 on v0

v1 whole, which is shorter than its diff:
```python
import jax
import jax.numpy as jnp
from jax import lax
from jax.experimental import pallas as pl
from jax.experimental.pallas import tpu as pltpu
from jax.sharding import PartitionSpec as P


SHARES = (7, 6, 6, 7, 6, 6, 7, 6, 6, 7)
LAG = 3
VMEM = 12 * 2**20


def side(count):
    return max(i for i in range(1, count + 1) if i * i <= count and count % i == 0)


def halves(value):
    high = value.astype(jnp.bfloat16)
    return high, (value - high.astype(jnp.float32)).astype(jnp.bfloat16)


def pick(index, values):
    chosen = values[0]
    for i, value in enumerate(values[1:], 1):
        chosen = jnp.where(index == i, value, chosen)
    return chosen


def product_kernel(pieces, nx, sets, groups, *refs):
    parts, factors = refs[:pieces * nx], refs[pieces * nx:pieces * nx + 2 * nx * sets * groups]
    outs = refs[len(parts) + len(factors):]
    terms = [halves(part[...]) for part in parts]
    for f in range(sets):
        for g in range(groups):
            chosen = factors[2 * nx * (f * groups + g):]
            totals = [None] * pieces
            for s in range(nx):
                high, low = chosen[2 * s][...], chosen[2 * s + 1][...]
                for which, b in ((1, high), (0, low), (0, high)):
                    for i in range(pieces):
                        term = jnp.dot(terms[i * nx + s][which], b, preferred_element_type=jnp.float32)
                        totals[i] = term if totals[i] is None else totals[i] + term
            for i in range(pieces):
                out = outs[f * pieces + i]
                width = out.shape[1] // groups
                out[:, g * width:(g + 1) * width] = totals[i]


def product(pieces, sets):
    nx, groups = len(pieces[0]), len(sets[0])
    width = sets[0][0][0].shape[1] * groups
    whole = lambda value: pl.BlockSpec(value.shape, lambda i: (0, 0))
    flat = [part for piece in pieces for part in piece] + [term for each in sets for group in each for term in group]
    results = [jax.ShapeDtypeStruct((piece[0].shape[0], width), jnp.float32) for _ in sets for piece in pieces]
    flops = sum(6 * part.size * width * len(sets) for piece in pieces for part in piece)
    found = pl.pallas_call(
        lambda *refs: product_kernel(len(pieces), nx, len(sets), groups, *refs),
        grid=(1,),
        out_shape=results,
        in_specs=[whole(value) for value in flat],
        out_specs=[whole(result) for result in results],
        compiler_params=pltpu.CompilerParams(vmem_limit_bytes=VMEM),
        cost_estimate=pl.CostEstimate(flops=flops, bytes_accessed=flops // 3072, transcendentals=0),
        name="product",
    )(*flat)
    return [found[f * len(pieces):(f + 1) * len(pieces)] for f in range(len(sets))]


def solution(mesh):
    layers, rows, cols = (mesh.shape[a] for a in ("layer", "row", "col"))
    nx = side(cols)
    ny = cols // nx
    if rows % ny or layers != 4:
        raise ValueError("mesh")
    q = rows // ny

    def along_x(shift):
        return [(y * nx + x, y * nx + (x + shift) % nx) for y in range(ny) for x in range(nx)]

    def along_y(shift):
        return [(y * nx + x, (y + shift) % ny * nx + x) for y in range(ny) for x in range(nx)]

    turn = [
        ((r * ny + y) * nx + x, ((y * q + r % q) * ny + r // q) * nx + x)
        for r in range(rows) for y in range(ny) for x in range(nx) if r // q != y
    ]
    pairs = [(0, 1), (1, 0), (2, 3), (3, 2)]
    across = [(1, 2), (2, 1)]

    def add(a, b):
        return a + b

    def body(panels, eigvecs):
        layer, row = lax.axis_index("layer"), lax.axis_index("row")
        col = lax.axis_index("col")
        y, x = col // nx, col % nx
        end = (layer == 0) | (layer == layers - 1)
        depth = panels.shape[1]
        width = eigvecs.shape[1]
        groups = 2 if width % 256 == 0 else 1
        unit = panels.shape[0] // sum(SHARES)
        n = len(SHARES)
        pieces, at = [], 0
        for share in SHARES:
            pieces.append(panels[at:at + share * unit])
            at += share * unit

        own = [eigvecs[:, g * width // groups:(g + 1) * width // groups] for g in range(groups)]
        own = [lax.optimization_barrier(part) for part in own]
        stays = row // q == y
        turned = [lax.ppermute(own[g], ("row", "col"), turn) for g in range(groups)]
        gathered = {}

        def gather(i):
            gathered[i] = [lax.ppermute(pieces[i], "col", along_x(s)) for s in range(1, nx)]

        for i in range(n):
            gather(i)

        def arrange(blocks):
            count = eigvecs.shape[0] // depth
            chunks = [[block[c * depth:(c + 1) * depth] for c in range(count)] for block in blocks]
            by_y = []
            for t in range(ny):
                terms = []
                for s in range(nx):
                    k, found = (x - s) % nx, []
                    for m in range(q):
                        back = (row - (y + t) % ny * q - m) % rows
                        found += [pick(back, [chunk[c] for chunk in chunks]) for c in range(count)]
                    value = pick(k, found)
                    high = lax.reduce_precision(value, 8, 7)
                    terms += [high.astype(jnp.bfloat16), (value - high).astype(jnp.bfloat16)]
                by_y.append(terms)
            return by_y

        factors = []
        parts = [[piece] + gathered[i] for i, piece in enumerate(pieces)]
        first = [[] for _ in range(1, ny)]
        for g in range(groups):
            held = jnp.where(stays, own[g], turned[g])
            blocks = [held] + [
                lax.ppermute(held, "row", [(r, (r + s) % rows) for r in range(rows)]) for s in range(1, rows)
            ]
            factors.append(arrange(blocks))
            for t in range(1, ny):
                value = product([parts[0]], [[factors[g][t]]])[0][0]
                first[t - 1].append(lax.ppermute(value, "col", along_y(t)))
        near = [product([parts[0]], [[group[0] for group in factors]])[0][0]]
        sent = [[jnp.concatenate(pair, axis=1) for pair in first]]
        starts = [unit * sum(SHARES[:i]) for i in range(n)]
        result = jnp.zeros((panels.shape[0], width), jnp.float32)
        total, summed, done, paired, crossed = {}, {}, {}, {}, {}
        for i in range(n + LAG + 2):
            if i % 2 == 0 and i + 1 < n:
                both = parts[i + 1:i + 3]
                found = product(both, [[group[t] for group in factors] for t in range(ny)])
                near += found[0]
                for k in range(len(both)):
                    sent.append([lax.ppermute(found[t][k], "col", along_y(t)) for t in range(1, ny)])
            if i < n:
                total[i] = near[i]
                for part in sent[i]:
                    total[i] = add(total[i], part)
            if LAG <= i < n + LAG:
                done[i - LAG] = add(summed[i - LAG], crossed[i - LAG])
            if i < n + LAG:
                if i < LAG:
                    give = total[i]
                elif i >= n:
                    give = done[i - LAG]
                else:
                    give = jnp.where(end, total[i], done[i - LAG])
                paired[i] = lax.ppermute(give, "layer", pairs)
            k = i - 1
            if 0 <= k < n:
                summed[k] = add(total[k], paired[k])
                crossed[k] = lax.ppermute(summed[k], "layer", across)
            k = i - LAG - 1
            if 0 <= k < n:
                value = jnp.where(end, paired[k + LAG], done[k])
                result = lax.dynamic_update_slice(result, value, (starts[k], 0))
        return result

    in_specs = (P("row", ("layer", "col")), P(("layer", "row"), "col"))
    out_specs = P("row", "col")
    step = jax.shard_map(body, mesh=mesh, in_specs=in_specs, out_specs=out_specs, check_vma=False)

    def traced(panels, eigvecs):
        jax.eval_shape(step, panels, eigvecs)
        return step(panels, eigvecs)

    return traced
```

time: 384 us -> 251 us (0.65)
  waiting for transfers between devices: 334 us -> 101 us
  starting transfers between devices: 0.08 us -> 104 us
  matrix products: 31.9 us -> 0 us
  Pallas kernels: 0 us -> 20.3 us
  other arithmetic: 0 us -> 14.7 us
  between operations: 13.1 us -> 0.63 us
  local copies, waits for them, and re-layouts: 4.64 us -> 9.54 us
    all_gather x2 -> x0, waiting for transfers between devices: 178 us -> none  [the longest x1 160 us: local(): lax.all_gather(panels, 'col', axis=1, tiled=True)]
    psum x1 -> x0, waiting for transfers between devices: 155 us -> none  [local(): result = lax.psum(partial_sum, 'layer')]
    ppermute x0 -> x48, starting transfers between devices: none -> 104 us  [the longest x13 48.2 us: body(): paired[i] = lax.ppermute(give, 'layer', pairs)]
    ppermute x0 -> x48, waiting for transfers between devices: none -> 101 us  [the longest x9 35.4 us: body(): lax.ppermute(found[t][k], 'col', along_y(t))]
    dot_general x1 -> x0, matrix products: 31.9 us -> none  [local(): jnp.dot(lax.all_gather(panels, 'col', axis=1, tiled=True), layer_vecs, pr...]
    pallas_call x0 -> x8, Pallas kernels: none -> 20.3 us  [product(): pl.pallas_call(lambda *refs: product_kernel(len(pieces), nx, len(sets), g...]
    select_n x0 -> x9, other arithmetic: none -> 5.53 us  [the longest x2 2.88 us: body(): held = jnp.where(stays, own[g], turned[g])]
    add x0 -> x16, other arithmetic: none -> 4.36 us  [add(): return a + b]
  transfers between devices with their start and end apart: 3 -> 48, of which waited for: 3 -> 21; matrix products, arithmetic and copies ran while one was open for 0% -> 7% of each run, Pallas kernels for 0% -> 8%
where the time goes in v1:
time: 251 us; the launch traced here: 250 us
  starting transfers between devices  104 us (41%)
  waiting for transfers between devices  101 us (40%)
  Pallas kernels  20.3 us (8%)
  other arithmetic  14.7 us (6%)
  local copies, waits for them, and re-layouts  9.54 us (4%)
    ppermute x13, starting transfers between devices, body(): paired[i] = lax.ppermute(give, 'layer', pairs)  48.2 us
    ppermute x9, waiting for transfers between devices, body(): lax.ppermute(found[t][k], 'col', along_y(t))  35.4 us
    ppermute x13, waiting for transfers between devices, body(): paired[i] = lax.ppermute(give, 'layer', pairs)  31.2 us
    ppermute x10, waiting for transfers between devices, gather(): lax.ppermute(pieces[i], 'col', along_x(s))  30.3 us
    ppermute x2, starting transfers between devices, body(): lax.ppermute(held, 'row', [(r, (r + s) % rows) for r in range(rows)])  24 us
    pallas_call x8, Pallas kernels, product(): pl.pallas_call(lambda *refs: product_kernel(len(pieces), nx, len(sets), g...  20.3 us
    ppermute x10, starting transfers between devices, gather(): lax.ppermute(pieces[i], 'col', along_x(s))  12 us
    ppermute x10, starting transfers between devices, body(): crossed[k] = lax.ppermute(summed[k], 'layer', across)  7.6 us
  transfers between devices with their start and end apart: 48, of which 21 were waited for; matrix products, arithmetic and copies ran while one was open for 7% of the time, Pallas kernels for 8%

profile of v1, /device:TPU:0, one launch (start us, length us, event | category | flops | bytes accessed | tf_op | source)
XLA Modules:
  0.0 250.4 jit_solution(9997668396733188773)
XLA Ops:
  6.6 14.1 %collective-permute-start.3 = (f32[1024,256]{1,0:T(8,128)S(1)}, f32[1024,256]{1,0:T(8,128)}, u32[]{:S(2)}, u32[]{:S(2)}) collective-permute-start(f32[1024,256]{1,0:T(8,128)S(1)} %broadcast_select_fusion.1), channel_id=1, source_target_pairs={{0,4},{4,0},{1,5},{5,1},{2,6},{6,2},{3,7},{7,3},{8,12},{12,8},{9,1... | collective-permute-start | bytes 3145736 | tf_op jit(solution)/shard_map/ppermute | solution.py:144
  22.1 9.8 %collective-permute-start.5 = (f32[1024,256]{1,0:T(8,128)S(1)}, f32[1024,256]{1,0:T(8,128)}, u32[]{:S(2)}, u32[]{:S(2)}) collective-permute-start(f32[1024,256]{1,0:T(8,128)S(1)} %broadcast_select_fusion), channel_id=1, source_target_pairs={{0,4},{4,0},{1,5},{5,1},{2,6},{6,2},{3,7},{7,3},{8,12},{12,8},{9,1... | collective-permute-start | bytes 3145736 | tf_op jit(solution)/shard_map/ppermute | solution.py:144
  40.6 16.0 %collective-permute-done.7.refs_1_ = f32[224,512]{1,0:T(8,128)S(1)} collective-permute-done((f32[224,512]{1,0:T(8,128)S(1)}, f32[224,512]{1,0:T(8,128)S(1)}, u32[]{:S(2)}, u32[]{:S(2)}) %collective-permute-start.7) | collective-permute-done | bytes 458784 | tf_op jit(solution)/shard_map/ppermute | solution.py:116
  62.7 2.3 collective-permute-done.8
  70.2 3.3 %collective-permute-done.14.refs_1_ = f32[192,512]{1,0:T(8,128)S(1)} collective-permute-done((f32[192,512]{1,0:T(8,128)}, f32[192,512]{1,0:T(8,128)S(1)}, u32[]{:S(2)}, u32[]{:S(2)}) %collective-permute-start.14) | collective-permute-done | bytes 393248 | tf_op jit(solution)/shard_map/ppermute | solution.py:116
  73.4 3.8 %product.12 = (f32[192,512]{1,0:T(8,128)S(1)}, f32[192,512]{1,0:T(8,128)S(1)}, f32[192,512]{1,0:T(8,128)S(1)}, f32[192,512]{1,0:T(8,128)S(1)}) custom-call(f32[192,512]{1,0:T(8,128)} %get-tuple-element.82.refs_0_, f32[192,512]{1,0:T(8,128)S(1)} %collective-permute-done.14.refs_1_, f32[192,512]{1,0:T(8,128)} %get-tuple-element.81.refs_2_, ...), custom_call_target="tpu_custom_call" | custom-call | flops 2415919104 | bytes 786432 | tf_op jit(solution)/shard_map/product/pallas_call | solution.py:57
  81.1 4.8 %product.8 = (f32[224,512]{1,0:T(8,128)S(1)}, f32[192,512]{1,0:T(8,128)S(1)}, f32[224,512]{1,0:T(8,128)}, f32[192,512]{1,0:T(8,128)S(1)}) custom-call(f32[224,512]{1,0:T(8,128)} %get-tuple-element.77.refs_0_, f32[224,512]{1,0:T(8,128)} %collective-permute-done.refs_1_, f32[192,512]{1,0:T(8,128)S(1)} %copy-done.15, ...), custom_call_target="tpu_custom_call" | custom-call | flops 2617245696 | bytes 851968 | tf_op jit(solution)/shard_map/product/pallas_call | solution.py:57
  94.5 4.7 %collective-permute-done.23 = f32[192,512]{1,0:T(8,128)S(1)} collective-permute-done((f32[192,512]{1,0:T(8,128)S(1)}, f32[192,512]{1,0:T(8,128)S(1)}, u32[]{:S(2)}, u32[]{:S(2)}) %collective-permute-start.23) | collective-permute-done | bytes 393248 | tf_op jit(solution)/shard_map/ppermute | solution.py:161
  108.6 2.1 collective-permute-start.17
  112.3 2.3 collective-permute-done.38.refs_1_
  114.6 3.9 %collective-permute-start.24 = (f32[192,512]{1,0:T(8,128)S(1)}, f32[192,512]{1,0:T(8,128)S(1)}, u32[]{:S(2)}, u32[]{:S(2)}) collective-permute-start(f32[192,512]{1,0:T(8,128)S(1)} %add.158), channel_id=1, source_target_pairs={{0,8},{8,0},{16,24},{24,16},{1,9},{9,1},{17,25},{25,17},{2,10},{10... | collective-permute-start | bytes 1179656 | tf_op jit(solution)/shard_map/ppermute | solution.py:175
  118.5 6.0 %collective-permute-done.21.refs_3_ = f32[224,512]{1,0:T(8,128)} collective-permute-done((f32[224,512]{1,0:T(8,128)}, f32[224,512]{1,0:T(8,128)}, u32[]{:S(2)}, u32[]{:S(2)}) %collective-permute-start.21) | collective-permute-done | bytes 458784 | tf_op jit(solution)/shard_map/ppermute | solution.py:116
  124.4 3.9 %collective-permute-start.12 = (f32[224,512]{1,0:T(8,128)S(1)}, f32[224,512]{1,0:T(8,128)S(1)}, u32[]{:S(2)}, u32[]{:S(2)}) collective-permute-start(f32[224,512]{1,0:T(8,128)S(1)} %get-tuple-element.59), channel_id=1, source_target_pairs={{0,8},{8,0},{16,24},{24,16},{1,9},{9,1},{17,25},{25,17},{2,10},{10... | collective-permute-start | bytes 1376264 | tf_op jit(solution)/shard_map/ppermute | solution.py:175
  128.3 4.2 %product.13 = (f32[192,512]{1,0:T(8,128)S(1)}, f32[224,512]{1,0:T(8,128)S(1)}, f32[192,512]{1,0:T(8,128)S(1)}, f32[224,512]{1,0:T(8,128)S(1)}) custom-call(f32[192,512]{1,0:T(8,128)} %get-tuple-element.80.refs_0_, f32[192,512]{1,0:T(8,128)} %collective-permute-done.20.refs_1_, f32[224,512]{1,0:T(8,128)} %get-tuple-element.75.refs_2_, ...), custom_call_target="tpu_custom_call" | custom-call | flops 2617245696 | bytes 851968 | tf_op jit(solution)/shard_map/product/pallas_call | solution.py:57
  132.6 2.9 %product.15 = (f32[224,512]{1,0:T(8,128)S(1)}, f32[224,512]{1,0:T(8,128)S(1)}) custom-call(f32[224,512]{1,0:T(8,128)} %get-tuple-element.74.refs_0_, f32[224,512]{1,0:T(8,128)} %collective-permute-done.38.refs_1_, bf16[512,256]{1,0:T(8,128)(2,1)S(1)} %copy-done.5, bf16[512,256]{1,0:T(8,128)(2,1)S(1)} %copy-done.3, bf16[512,256]{1,0:T(8,128)(2,1)S(1)} %copy-done.1, ...), custom_call_target="tpu_custom_call" | custom-call | flops 1409286144 | bytes 458752 | tf_op jit(solution)/shard_map/product/pallas_call | solution.py:57
  135.7 2.0 collective-permute-start.13
  140.1 2.7 %product.14 = (f32[192,512]{1,0:T(8,128)S(1)}, f32[192,512]{1,0:T(8,128)S(1)}, f32[192,512]{1,0:T(8,128)S(1)}, f32[192,512]{1,0:T(8,128)S(1)}) custom-call(f32[192,512]{1,0:T(8,128)S(1)} %copy-done.14, f32[192,512]{1,0:T(8,128)S(1)} %collective-permute-done.30.refs_1_, f32[192,512]{1,0:T(8,128)S(1)} %copy-done.13, ...), custom_call_target="tpu_custom_call" | custom-call | flops 2415919104 | bytes 786432 | tf_op jit(solution)/shard_map/product/pallas_call | solution.py:57
  144.0 13.4 %collective-permute-done.13 = f32[192,512]{1,0:T(8,128)S(1)} collective-permute-done((f32[192,512]{1,0:T(8,128)S(1)}, f32[192,512]{1,0:T(8,128)S(1)}, u32[]{:S(2)}, u32[]{:S(2)}) %collective-permute-start.13) | collective-permute-done | bytes 393248 | tf_op jit(solution)/shard_map/ppermute | solution.py:161
  158.3 7.5 %collective-permute-done.22 = f32[192,512]{1,0:T(8,128)S(1)} collective-permute-done((f32[192,512]{1,0:T(8,128)S(1)}, f32[192,512]{1,0:T(8,128)S(1)}, u32[]{:S(2)}, u32[]{:S(2)}) %collective-permute-start.22) | collective-permute-done | bytes 393248 | tf_op jit(solution)/shard_map/ppermute | solution.py:161
  166.6 9.0 %collective-permute-done.27 = f32[224,512]{1,0:T(8,128)S(1)} collective-permute-done((f32[224,512]{1,0:T(8,128)S(1)}, f32[224,512]{1,0:T(8,128)S(1)}, u32[]{:S(2)}, u32[]{:S(2)}) %collective-permute-start.27) | collective-permute-done | bytes 458784 | tf_op jit(solution)/shard_map/ppermute | solution.py:161
  178.1 8.9 %collective-permute-done.26 = f32[192,512]{1,0:T(8,128)S(1)} collective-permute-done((f32[192,512]{1,0:T(8,128)S(1)}, f32[192,512]{1,0:T(8,128)S(1)}, u32[]{:S(2)}, u32[]{:S(2)}) %collective-permute-start.26) | collective-permute-done | bytes 393248 | tf_op jit(solution)/shard_map/ppermute | solution.py:175
  187.8 4.1 %collective-permute-done.29 = f32[224,512]{1,0:T(8,128)S(1)} collective-permute-done((f32[224,512]{1,0:T(8,128)S(1)}, f32[224,512]{1,0:T(8,128)S(1)}, u32[]{:S(2)}, u32[]{:S(2)}) %collective-permute-start.29) | collective-permute-done | bytes 458784 | tf_op jit(solution)/shard_map/ppermute | solution.py:175
  193.6 7.5 %collective-permute-start.34 = (f32[192,512]{1,0:T(8,128)S(1)}, f32[192,512]{1,0:T(8,128)S(1)}, u32[]{:S(2)}, u32[]{:S(2)}) collective-permute-start(f32[192,512]{1,0:T(8,128)S(1)} %get-tuple-element.47), channel_id=1, source_target_pairs={{0,8},{8,0},{16,24},{24,16},{1,9},{9,1},{17,25},{25,17},{2,10},{10... | collective-permute-start | bytes 1179656 | tf_op jit(solution)/shard_map/ppermute | solution.py:175
  201.3 7.4 %collective-permute-start.37 = (f32[192,512]{1,0:T(8,128)S(1)}, f32[192,512]{1,0:T(8,128)S(1)}, u32[]{:S(2)}, u32[]{:S(2)}) collective-permute-start(f32[192,512]{1,0:T(8,128)S(1)} %get-tuple-element.44), channel_id=1, source_target_pairs={{0,8},{8,0},{16,24},{24,16},{1,9},{9,1},{17,25},{25,17},{2,10},{10... | collective-permute-start | bytes 1179656 | tf_op jit(solution)/shard_map/ppermute | solution.py:175
  208.9 5.5 %collective-permute-start.41 = (f32[224,512]{1,0:T(8,128)S(1)}, f32[224,512]{1,0:T(8,128)S(1)}, u32[]{:S(2)}, u32[]{:S(2)}) collective-permute-start(f32[224,512]{1,0:T(8,128)S(1)} %get-tuple-element.41), channel_id=1, source_target_pairs={{0,8},{8,0},{16,24},{24,16},{1,9},{9,1},{17,25},{25,17},{2,10},{10... | collective-permute-start | bytes 1376264 | tf_op jit(solution)/shard_map/ppermute | solution.py:175
  215.2 2.7 %collective-permute-done.37 = f32[192,512]{1,0:T(8,128)S(1)} collective-permute-done((f32[192,512]{1,0:T(8,128)S(1)}, f32[192,512]{1,0:T(8,128)S(1)}, u32[]{:S(2)}, u32[]{:S(2)}) %collective-permute-start.37) | collective-permute-done | bytes 393248 | tf_op jit(solution)/shard_map/ppermute | solution.py:175
  218.8 4.9 %collective-permute-done.41 = f32[224,512]{1,0:T(8,128)S(1)} collective-permute-done((f32[224,512]{1,0:T(8,128)S(1)}, f32[224,512]{1,0:T(8,128)S(1)}, u32[]{:S(2)}, u32[]{:S(2)}) %collective-permute-start.41) | collective-permute-done | bytes 458784 | tf_op jit(solution)/shard_map/ppermute | solution.py:175
  224.6 4.0 %collective-permute-start.43 = (f32[192,512]{1,0:T(8,128)S(1)}, f32[192,512]{1,0:T(8,128)S(1)}, u32[]{:S(2)}, u32[]{:S(2)}) collective-permute-start(f32[192,512]{1,0:T(8,128)S(1)} %add.174), channel_id=1, source_target_pairs={{0,8},{8,0},{16,24},{24,16},{1,9},{9,1},{17,25},{25,17},{2,10},{10... | collective-permute-start | bytes 1179656 | tf_op jit(solution)/shard_map/ppermute | solution.py:175
  228.6 6.7 %collective-permute-start.45 = (f32[192,512]{1,0:T(8,128)S(1)}, f32[192,512]{1,0:T(8,128)S(1)}, u32[]{:S(2)}, u32[]{:S(2)}) collective-permute-start(f32[192,512]{1,0:T(8,128)S(1)} %add.176), channel_id=1, source_target_pairs={{0,8},{8,0},{16,24},{24,16},{1,9},{9,1},{17,25},{25,17},{2,10},{10... | collective-permute-start | bytes 1179656 | tf_op jit(solution)/shard_map/ppermute | solution.py:175
  235.3 4.9 %collective-permute-start.47 = (f32[224,512]{1,0:T(8,128)S(1)}, f32[224,512]{1,0:T(8,128)S(1)}, u32[]{:S(2)}, u32[]{:S(2)}) collective-permute-start(f32[224,512]{1,0:T(8,128)S(1)} %add.178), channel_id=1, source_target_pairs={{0,8},{8,0},{16,24},{24,16},{1,9},{9,1},{17,25},{25,17},{2,10},{10... | collective-permute-start | bytes 1376264 | tf_op jit(solution)/shard_map/ppermute | solution.py:175
  240.3 4.4 %collective-permute-done.45 = f32[192,512]{1,0:T(8,128)S(1)} collective-permute-done((f32[192,512]{1,0:T(8,128)S(1)}, f32[192,512]{1,0:T(8,128)S(1)}, u32[]{:S(2)}, u32[]{:S(2)}) %collective-permute-start.45) | collective-permute-done | bytes 393248 | tf_op jit(solution)/shard_map/ppermute | solution.py:175
  244.7 4.8 %collective-permute-done.47 = f32[224,512]{1,0:T(8,128)S(1)} collective-permute-done((f32[224,512]{1,0:T(8,128)S(1)}, f32[224,512]{1,0:T(8,128)S(1)}, u32[]{:S(2)}, u32[]{:S(2)}) %collective-permute-start.47) | collective-permute-done | bytes 458784 | tf_op jit(solution)/shard_map/ppermute | solution.py:175
  (172 shorter events, 65.4 us)
Async XLA Ops:
  3.4 17.3 %collective-permute-start.4 = (f32[1024,256]{1,0:T(8,128)S(1)}, f32[1024,256]{1,0:T(8,128)}, u32[]{:S(2)}, u32[]{:S(2)}) collective-permute-start(f32[1024,256]{1,0:T(8,128)S(1)} %get-tuple-element.90), channel_id=1, source_target_pairs={{2,4},{3,5},{4,2},{5,3},{10,12},{11,13},{12,10},{13,11},{18,20},{1... | collective-permute-start | bytes 3145736 | tf_op jit(solution)/shard_map/ppermute | solution.py:112
  6.6 31.5 %collective-permute-start.3 = (f32[1024,256]{1,0:T(8,128)S(1)}, f32[1024,256]{1,0:T(8,128)}, u32[]{:S(2)}, u32[]{:S(2)}) collective-permute-start(f32[1024,256]{1,0:T(8,128)S(1)} %broadcast_select_fusion.1), channel_id=1, source_target_pairs={{0,4},{4,0},{1,5},{5,1},{2,6},{6,2},{3,7},{7,3},{8,12},{12,8},{9,1... | collective-permute-start | bytes 3145736 | tf_op jit(solution)/shard_map/ppermute | solution.py:144
  22.1 36.8 %collective-permute-start.5 = (f32[1024,256]{1,0:T(8,128)S(1)}, f32[1024,256]{1,0:T(8,128)}, u32[]{:S(2)}, u32[]{:S(2)}) collective-permute-start(f32[1024,256]{1,0:T(8,128)S(1)} %broadcast_select_fusion), channel_id=1, source_target_pairs={{0,4},{4,0},{1,5},{5,1},{2,6},{6,2},{3,7},{7,3},{8,12},{12,8},{9,1... | collective-permute-start | bytes 3145736 | tf_op jit(solution)/shard_map/ppermute | solution.py:144
  33.1 47.9 %collective-permute-start = (f32[224,512]{1,0:T(8,128)}, f32[224,512]{1,0:T(8,128)}, u32[]{:S(2)}, u32[]{:S(2)}) collective-permute-start(f32[224,512]{1,0:T(8,128)} %get-tuple-element.77.refs_0_), channel_id=1, source_target_pairs={{0,1},{1,0},{2,3},{3,2},{4,5},{5,4},{6,7},{7,6},{8,9},{9,8},{10,11... | collective-permute-start | bytes 1376264 | tf_op jit(solution)/shard_map/ppermute | solution.py:116
  34.6 21.9 %collective-permute-start.7 = (f32[224,512]{1,0:T(8,128)S(1)}, f32[224,512]{1,0:T(8,128)S(1)}, u32[]{:S(2)}, u32[]{:S(2)}) collective-permute-start(f32[224,512]{1,0:T(8,128)S(1)} %get-tuple-element.76.refs_0_), channel_id=1, source_target_pairs={{0,1},{1,0},{2,3},{3,2},{4,5},{5,4},{6,7},{7,6},{8,9},{9,8},{10,11... | collective-permute-start | bytes 1376264 | tf_op jit(solution)/shard_map/ppermute | solution.py:116
  36.6 33.6 %collective-permute-start.15 = (f32[192,512]{1,0:T(8,128)}, f32[192,512]{1,0:T(8,128)}, u32[]{:S(2)}, u32[]{:S(2)}) collective-permute-start(f32[192,512]{1,0:T(8,128)} %get-tuple-element.81.refs_2_), channel_id=1, source_target_pairs={{0,1},{1,0},{2,3},{3,2},{4,5},{5,4},{6,7},{7,6},{8,9},{9,8},{10,11... | collective-permute-start | bytes 1179656 | tf_op jit(solution)/shard_map/ppermute | solution.py:116
  38.1 35.3 %collective-permute-start.14 = (f32[192,512]{1,0:T(8,128)}, f32[192,512]{1,0:T(8,128)S(1)}, u32[]{:S(2)}, u32[]{:S(2)}) collective-permute-start(f32[192,512]{1,0:T(8,128)} %get-tuple-element.82.refs_0_), channel_id=1, source_target_pairs={{0,1},{1,0},{2,3},{3,2},{4,5},{5,4},{6,7},{7,6},{8,9},{9,8},{10,11... | collective-permute-start | bytes 1179656 | tf_op jit(solution)/shard_map/ppermute | solution.py:116
  65.0 16.1 %collective-permute-start.1 = (f32[192,512]{1,0:T(8,128)S(1)}, f32[192,512]{1,0:T(8,128)S(1)}, u32[]{:S(2)}, u32[]{:S(2)}) collective-permute-start(f32[192,512]{1,0:T(8,128)S(1)} %copy-done.15), channel_id=1, source_target_pairs={{0,1},{1,0},{2,3},{3,2},{4,5},{5,4},{6,7},{7,6},{8,9},{9,8},{10,11... | collective-permute-start | bytes 1179656 | tf_op jit(solution)/shard_map/ppermute | solution.py:116
  68.5 21.7 %collective-permute-start.10 = (f32[224,512]{1,0:T(8,128)S(1)}, f32[224,512]{1,0:T(8,128)S(1)}, u32[]{:S(2)}, u32[]{:S(2)}) collective-permute-start(f32[224,512]{1,0:T(8,128)S(1)} %maximum_add_fusion), channel_id=1, source_target_pairs={{0,8},{8,0},{16,24},{24,16},{1,9},{9,1},{17,25},{25,17},{2,10},{10... | collective-permute-start | bytes 1376264 | tf_op jit(solution)/shard_map/ppermute | solution.py:175
  80.6 18.6 %collective-permute-start.23 = (f32[192,512]{1,0:T(8,128)S(1)}, f32[192,512]{1,0:T(8,128)S(1)}, u32[]{:S(2)}, u32[]{:S(2)}) collective-permute-start(f32[192,512]{1,0:T(8,128)S(1)} %get-tuple-element.32), channel_id=1, source_target_pairs={{0,2},{1,3},{2,0},{3,1},{4,6},{5,7},{6,4},{7,5},{8,10},{9,11},{10,... | collective-permute-start | bytes 1179656 | tf_op jit(solution)/shard_map/ppermute | solution.py:161
  88.3 18.8 %collective-permute-start.6 = (f32[224,512]{1,0:T(8,128)}, f32[224,512]{1,0:T(8,128)}, u32[]{:S(2)}, u32[]{:S(2)}) collective-permute-start(f32[224,512]{1,0:T(8,128)} %get-tuple-element.24), channel_id=1, source_target_pairs={{0,2},{1,3},{2,0},{3,1},{4,6},{5,7},{6,4},{7,5},{8,10},{9,11},{10,... | collective-permute-start | bytes 1376264 | tf_op jit(solution)/shard_map/ppermute | solution.py:161
  91.0 17.5 %collective-permute-start.11 = (f32[224,512]{1,0:T(8,128)}, f32[224,512]{1,0:T(8,128)}, u32[]{:S(2)}, u32[]{:S(2)}) collective-permute-start(f32[224,512]{1,0:T(8,128)} %add.151), channel_id=1, source_target_pairs={{8,16},{16,8},{9,17},{17,9},{10,18},{18,10},{11,19},{19,11},{12,20... | collective-permute-start | bytes 1376264 | tf_op jit(solution)/shard_map/ppermute | solution.py:179
  94.0 20.6 %collective-permute-start.38 = (f32[224,512]{1,0:T(8,128)}, f32[224,512]{1,0:T(8,128)}, u32[]{:S(2)}, u32[]{:S(2)}) collective-permute-start(f32[224,512]{1,0:T(8,128)} %get-tuple-element.74.refs_0_), channel_id=1, source_target_pairs={{0,1},{1,0},{2,3},{3,2},{4,5},{5,4},{6,7},{7,6},{8,9},{9,8},{10,11... | collective-permute-start | bytes 1376264 | tf_op jit(solution)/shard_map/ppermute | solution.py:116
  100.0 24.5 %collective-permute-start.21 = (f32[224,512]{1,0:T(8,128)}, f32[224,512]{1,0:T(8,128)}, u32[]{:S(2)}, u32[]{:S(2)}) collective-permute-start(f32[224,512]{1,0:T(8,128)} %get-tuple-element.75.refs_2_), channel_id=1, source_target_pairs={{0,1},{1,0},{2,3},{3,2},{4,5},{5,4},{6,7},{7,6},{8,9},{9,8},{10,11... | collective-permute-start | bytes 1376264 | tf_op jit(solution)/shard_map/ppermute | solution.py:116
  104.8 30.9 %collective-permute-start.31 = (f32[192,512]{1,0:T(8,128)}, f32[192,512]{1,0:T(8,128)S(1)}, u32[]{:S(2)}, u32[]{:S(2)}) collective-permute-start(f32[192,512]{1,0:T(8,128)} %get-tuple-element.78.refs_2_), channel_id=1, source_target_pairs={{0,1},{1,0},{2,3},{3,2},{4,5},{5,4},{6,7},{7,6},{8,9},{9,8},{10,11... | collective-permute-start | bytes 1179656 | tf_op jit(solution)/shard_map/ppermute | solution.py:116
  107.1 32.3 %collective-permute-start.30 = (f32[192,512]{1,0:T(8,128)}, f32[192,512]{1,0:T(8,128)S(1)}, u32[]{:S(2)}, u32[]{:S(2)}) collective-permute-start(f32[192,512]{1,0:T(8,128)} %get-tuple-element.79.refs_0_), channel_id=1, source_target_pairs={{0,1},{1,0},{2,3},{3,2},{4,5},{5,4},{6,7},{7,6},{8,9},{9,8},{10,11... | collective-permute-start | bytes 1179656 | tf_op jit(solution)/shard_map/ppermute | solution.py:116
  108.6 26.9 %collective-permute-start.17 = (f32[192,512]{1,0:T(8,128)S(1)}, f32[192,512]{1,0:T(8,128)S(1)}, u32[]{:S(2)}, u32[]{:S(2)}) collective-permute-start(f32[192,512]{1,0:T(8,128)S(1)} %add.154), channel_id=1, source_target_pairs={{0,8},{8,0},{16,24},{24,16},{1,9},{9,1},{17,25},{25,17},{2,10},{10... | collective-permute-start | bytes 1179656 | tf_op jit(solution)/shard_map/ppermute | solution.py:175
  114.6 28.1 %collective-permute-start.24 = (f32[192,512]{1,0:T(8,128)S(1)}, f32[192,512]{1,0:T(8,128)S(1)}, u32[]{:S(2)}, u32[]{:S(2)}) collective-permute-start(f32[192,512]{1,0:T(8,128)S(1)} %add.158), channel_id=1, source_target_pairs={{0,8},{8,0},{16,24},{24,16},{1,9},{9,1},{17,25},{25,17},{2,10},{10... | collective-permute-start | bytes 1179656 | tf_op jit(solution)/shard_map/ppermute | solution.py:175
  124.4 18.7 %collective-permute-start.12 = (f32[224,512]{1,0:T(8,128)S(1)}, f32[224,512]{1,0:T(8,128)S(1)}, u32[]{:S(2)}, u32[]{:S(2)}) collective-permute-start(f32[224,512]{1,0:T(8,128)S(1)} %get-tuple-element.59), channel_id=1, source_target_pairs={{0,8},{8,0},{16,24},{24,16},{1,9},{9,1},{17,25},{25,17},{2,10},{10... | collective-permute-start | bytes 1376264 | tf_op jit(solution)/shard_map/ppermute | solution.py:175
  135.5 73.2 %collective-permute-start.39 = (f32[224,512]{1,0:T(8,128)S(1)}, f32[224,512]{1,0:T(8,128)S(1)}, u32[]{:S(2)}, u32[]{:S(2)}) collective-permute-start(f32[224,512]{1,0:T(8,128)S(1)} %get-tuple-element.40), channel_id=1, source_target_pairs={{0,2},{1,3},{2,0},{3,1},{4,6},{5,7},{6,4},{7,5},{8,10},{9,11},{10,... | collective-permute-start | bytes 1376264 | tf_op jit(solution)/shard_map/ppermute | solution.py:161
  135.7 21.6 %collective-permute-start.13 = (f32[192,512]{1,0:T(8,128)S(1)}, f32[192,512]{1,0:T(8,128)S(1)}, u32[]{:S(2)}, u32[]{:S(2)}) collective-permute-start(f32[192,512]{1,0:T(8,128)S(1)} %copy-done.21), channel_id=1, source_target_pairs={{0,2},{1,3},{2,0},{3,1},{4,6},{5,7},{6,4},{7,5},{8,10},{9,11},{10,... | collective-permute-start | bytes 1179656 | tf_op jit(solution)/shard_map/ppermute | solution.py:161
  139.4 18.1 %collective-permute-start.18 = (f32[192,512]{1,0:T(8,128)S(1)}, f32[192,512]{1,0:T(8,128)S(1)}, u32[]{:S(2)}, u32[]{:S(2)}) collective-permute-start(f32[192,512]{1,0:T(8,128)S(1)} %add.155), channel_id=1, source_target_pairs={{8,16},{16,8},{9,17},{17,9},{10,18},{18,10},{11,19},{19,11},{12,20... | collective-permute-start | bytes 1179656 | tf_op jit(solution)/shard_map/ppermute | solution.py:179
  142.8 23.0 %collective-permute-start.22 = (f32[192,512]{1,0:T(8,128)S(1)}, f32[192,512]{1,0:T(8,128)S(1)}, u32[]{:S(2)}, u32[]{:S(2)}) collective-permute-start(f32[192,512]{1,0:T(8,128)S(1)} %get-tuple-element.30), channel_id=1, source_target_pairs={{0,2},{1,3},{2,0},{3,1},{4,6},{5,7},{6,4},{7,5},{8,10},{9,11},{10,... | collective-permute-start | bytes 1179656 | tf_op jit(solution)/shard_map/ppermute | solution.py:161
  143.2 22.7 %collective-permute-start.25 = (f32[192,512]{1,0:T(8,128)S(1)}, f32[192,512]{1,0:T(8,128)S(1)}, u32[]{:S(2)}, u32[]{:S(2)}) collective-permute-start(f32[192,512]{1,0:T(8,128)S(1)} %add.159), channel_id=1, source_target_pairs={{8,16},{16,8},{9,17},{17,9},{10,18},{18,10},{11,19},{19,11},{12,20... | collective-permute-start | bytes 1179656 | tf_op jit(solution)/shard_map/ppermute | solution.py:179
  157.4 18.3 %collective-permute-start.27 = (f32[224,512]{1,0:T(8,128)S(1)}, f32[224,512]{1,0:T(8,128)S(1)}, u32[]{:S(2)}, u32[]{:S(2)}) collective-permute-start(f32[224,512]{1,0:T(8,128)S(1)} %get-tuple-element.34), channel_id=1, source_target_pairs={{0,2},{1,3},{2,0},{3,1},{4,6},{5,7},{6,4},{7,5},{8,10},{9,11},{10,... | collective-permute-start | bytes 1376264 | tf_op jit(solution)/shard_map/ppermute | solution.py:161
  157.5 18.3 %collective-permute-start.28 = (f32[224,512]{1,0:T(8,128)S(1)}, f32[224,512]{1,0:T(8,128)S(1)}, u32[]{:S(2)}, u32[]{:S(2)}) collective-permute-start(f32[224,512]{1,0:T(8,128)S(1)} %get-tuple-element.108), channel_id=1, source_target_pairs={{8,16},{16,8},{9,17},{17,9},{10,18},{18,10},{11,19},{19,11},{12,20... | collective-permute-start | bytes 1376264 | tf_op jit(solution)/shard_map/ppermute | solution.py:179
  165.8 26.9 %collective-permute-start.32 = (f32[192,512]{1,0:T(8,128)S(1)}, f32[192,512]{1,0:T(8,128)S(1)}, u32[]{:S(2)}, u32[]{:S(2)}) collective-permute-start(f32[192,512]{1,0:T(8,128)S(1)} %get-tuple-element.36), channel_id=1, source_target_pairs={{0,2},{1,3},{2,0},{3,1},{4,6},{5,7},{6,4},{7,5},{8,10},{9,11},{10,... | collective-permute-start | bytes 1179656 | tf_op jit(solution)/shard_map/ppermute | solution.py:161
  175.6 25.5 %collective-permute-start.35 = (f32[192,512]{1,0:T(8,128)S(1)}, f32[192,512]{1,0:T(8,128)S(1)}, u32[]{:S(2)}, u32[]{:S(2)}) collective-permute-start(f32[192,512]{1,0:T(8,128)S(1)} %get-tuple-element.38), channel_id=1, source_target_pairs={{0,2},{1,3},{2,0},{3,1},{4,6},{5,7},{6,4},{7,5},{8,10},{9,11},{10,... | collective-permute-start | bytes 1179656 | tf_op jit(solution)/shard_map/ppermute | solution.py:161
  192.8 15.9 %collective-permute-start.40 = (f32[224,512]{1,0:T(8,128)S(1)}, f32[224,512]{1,0:T(8,128)S(1)}, u32[]{:S(2)}, u32[]{:S(2)}) collective-permute-start(f32[224,512]{1,0:T(8,128)S(1)} %get-tuple-element.106), channel_id=1, source_target_pairs={{8,16},{16,8},{9,17},{17,9},{10,18},{18,10},{11,19},{19,11},{12,20... | collective-permute-start | bytes 1376264 | tf_op jit(solution)/shard_map/ppermute | solution.py:179
  193.6 20.8 %collective-permute-start.34 = (f32[192,512]{1,0:T(8,128)S(1)}, f32[192,512]{1,0:T(8,128)S(1)}, u32[]{:S(2)}, u32[]{:S(2)}) collective-permute-start(f32[192,512]{1,0:T(8,128)S(1)} %get-tuple-element.47), channel_id=1, source_target_pairs={{0,8},{8,0},{16,24},{24,16},{1,9},{9,1},{17,25},{25,17},{2,10},{10... | collective-permute-start | bytes 1179656 | tf_op jit(solution)/shard_map/ppermute | solution.py:175
  201.3 16.7 %collective-permute-start.37 = (f32[192,512]{1,0:T(8,128)S(1)}, f32[192,512]{1,0:T(8,128)S(1)}, u32[]{:S(2)}, u32[]{:S(2)}) collective-permute-start(f32[192,512]{1,0:T(8,128)S(1)} %get-tuple-element.44), channel_id=1, source_target_pairs={{0,8},{8,0},{16,24},{24,16},{1,9},{9,1},{17,25},{25,17},{2,10},{10... | collective-permute-start | bytes 1179656 | tf_op jit(solution)/shard_map/ppermute | solution.py:175
  228.6 16.0 %collective-permute-start.45 = (f32[192,512]{1,0:T(8,128)S(1)}, f32[192,512]{1,0:T(8,128)S(1)}, u32[]{:S(2)}, u32[]{:S(2)}) collective-permute-start(f32[192,512]{1,0:T(8,128)S(1)} %add.176), channel_id=1, source_target_pairs={{0,8},{8,0},{16,24},{24,16},{1,9},{9,1},{17,25},{25,17},{2,10},{10... | collective-permute-start | bytes 1179656 | tf_op jit(solution)/shard_map/ppermute | solution.py:175
  (47 other events, 667.2 us)

commit v2 on v1

v2 whole, which is shorter than its diff:
```python
import jax
import jax.numpy as jnp
from jax import lax
from jax.experimental import pallas as pl
from jax.experimental.pallas import tpu as pltpu
from jax.sharding import PartitionSpec as P


SHARES = (7, 6, 6, 7, 6, 6, 7, 6, 6, 7)
LAG = 3
EARLY = 5
LATE = {0: (5, 6), 1: (7,), 2: (8, 9, 10)}
WORK = {-2: (1,), -1: (2,), 1: (3,), 3: (4, 5), 5: (6, 7), 7: (8, 9), 8: (10,)}
VMEM = 12 * 2**20


def side(count):
    return max(i for i in range(1, count + 1) if i * i <= count and count % i == 0)


def halves(value):
    high = value.astype(jnp.bfloat16)
    return high, (value - high.astype(jnp.float32)).astype(jnp.bfloat16)


def product_kernel(pieces, nx, sets, groups, *refs):
    parts, factors = refs[:pieces * nx], refs[pieces * nx:pieces * nx + 2 * nx * sets * groups]
    outs = refs[len(parts) + len(factors):]
    terms = [halves(part[...]) for part in parts]
    for f in range(sets):
        for g in range(groups):
            chosen = factors[2 * nx * (f * groups + g):]
            totals = [None] * pieces
            for s in range(nx):
                high, low = chosen[2 * s][...], chosen[2 * s + 1][...]
                for which, b in ((1, high), (0, low), (0, high)):
                    for i in range(pieces):
                        term = jnp.dot(terms[i * nx + s][which], b, preferred_element_type=jnp.float32)
                        totals[i] = term if totals[i] is None else totals[i] + term
            for i in range(pieces):
                out = outs[f * pieces + i]
                width = out.shape[1] // groups
                out[:, g * width:(g + 1) * width] = totals[i]


def product(pieces, sets):
    nx, groups = len(pieces[0]), len(sets[0])
    width = sets[0][0][0].shape[1] * groups
    whole = lambda value: pl.BlockSpec(value.shape, lambda i: (0, 0))
    flat = [part for piece in pieces for part in piece] + [term for each in sets for group in each for term in group]
    results = [pltpu.VMEM((piece[0].shape[0], width), jnp.float32) for _ in sets for piece in pieces]
    flops = sum(6 * part.size * width * len(sets) for piece in pieces for part in piece)
    found = pl.pallas_call(
        lambda *refs: product_kernel(len(pieces), nx, len(sets), groups, *refs),
        grid=(1,),
        out_shape=results,
        in_specs=[whole(value) for value in flat],
        out_specs=[whole(result) for result in results],
        compiler_params=pltpu.CompilerParams(vmem_limit_bytes=VMEM),
        cost_estimate=pl.CostEstimate(flops=flops, bytes_accessed=flops // 3072, transcendentals=0),
        name="product",
    )(*flat)
    return [found[f * len(pieces):(f + 1) * len(pieces)] for f in range(len(sets))]


def arrange_kernel(nx, ny, depth, place, *refs):
    row, y, x = place[0], place[1], place[2]
    rows = len(refs) - 2 * nx * ny
    q = rows // ny
    for t in range(ny):
        for s in range(nx):
            value = None
            for back in range(rows):
                count = refs[back].shape[0] // depth
                index = (row - back + rows) % rows
                for c in range(count):
                    here = (index // q == (y + t) % ny) & ((index % q) * count + c == (x - s + nx) % nx)
                    chunk = refs[back][c * depth:(c + 1) * depth, :]
                    value = chunk if value is None else jnp.where(here, chunk, value)
            at = rows + 2 * (t * nx + s)
            refs[at][...], refs[at + 1][...] = halves(value)


def arrange(place, blocks, nx, ny, depth):
    width = blocks[0].shape[1]
    whole = lambda value: pl.BlockSpec(value.shape, lambda i: (0, 0))
    results = [pltpu.VMEM((depth, width), jnp.bfloat16)] * (2 * nx * ny)
    found = pl.pallas_call(
        lambda *refs: arrange_kernel(nx, ny, depth, *refs),
        grid=(1,),
        out_shape=results,
        in_specs=[pl.BlockSpec(memory_space=pltpu.SMEM)] + [whole(block) for block in blocks],
        out_specs=[whole(result) for result in results],
        compiler_params=pltpu.CompilerParams(vmem_limit_bytes=VMEM),
        cost_estimate=pl.CostEstimate(flops=blocks[0].size * 64, bytes_accessed=blocks[0].size * 16, transcendentals=0),
        name="arrange",
    )(place, *blocks)
    return [found[2 * nx * t:2 * nx * (t + 1)] for t in range(ny)]


def combine_kernel(counts, flag, *refs):
    ins, outs = refs[:sum(counts)], refs[sum(counts):]
    found, at = [], 0
    for count in counts:
        total = ins[at][...]
        for ref in ins[at + 1:at + count]:
            total = total + ref[...]
        found.append(total)
        at += count
    for total, out in zip(found, outs):
        out[...] = total
    if len(counts) > 1:
        outs[-1][...] = jnp.where(flag[0] == 1, found[0], found[1])


def combine(flag, *lists):
    shape = lists[0][0].shape
    flat = [value for values in lists for value in values]
    whole = pl.BlockSpec(shape, lambda i: (0, 0))
    results = [pltpu.VMEM(shape, jnp.float32)] * (len(lists) + (len(lists) > 1))
    return pl.pallas_call(
        lambda *refs: combine_kernel([len(values) for values in lists], *refs),
        grid=(1,),
        out_shape=results,
        in_specs=[pl.BlockSpec(memory_space=pltpu.SMEM)] + [whole] * len(flat),
        out_specs=[whole] * len(results),
        compiler_params=pltpu.CompilerParams(vmem_limit_bytes=VMEM),
        cost_estimate=pl.CostEstimate(flops=flat[0].size * 64, bytes_accessed=flat[0].size * 16, transcendentals=0),
        name="combine",
    )(flag, *flat)


def solution(mesh):
    layers, rows, cols = (mesh.shape[a] for a in ("layer", "row", "col"))
    nx = side(cols)
    ny = cols // nx
    if rows % ny or layers != 4:
        raise ValueError("mesh")
    q = rows // ny

    def along_x(shift):
        return [(y * nx + x, y * nx + (x + shift) % nx) for y in range(ny) for x in range(nx)]

    def along_y(shift):
        return [(y * nx + x, (y + shift) % ny * nx + x) for y in range(ny) for x in range(nx)]

    turn = [
        ((r * ny + y) * nx + x, ((y * q + r % q) * ny + r // q) * nx + x)
        for r in range(rows) for y in range(ny) for x in range(nx) if r // q != y
    ]
    pairs = [(0, 1), (1, 0), (2, 3), (3, 2)]
    across = [(1, 2), (2, 1)]

    def body(panels, eigvecs):
        layer, row = lax.axis_index("layer"), lax.axis_index("row")
        col = lax.axis_index("col")
        y, x = col // nx, col % nx
        end = (layer == 0) | (layer == layers - 1)
        depth = panels.shape[1]
        width = eigvecs.shape[1]
        groups = 2 if width % 256 == 0 else 1
        unit = panels.shape[0] // sum(SHARES)
        n = len(SHARES)
        pieces, at = [], 0
        for share in SHARES:
            pieces.append(panels[at:at + share * unit])
            at += share * unit

        own, source = [], eigvecs
        for g in range(groups):
            own.append(lax.optimization_barrier(source[:, g * width // groups:(g + 1) * width // groups]))
            if g + 1 < groups:
                source, own[g] = lax.optimization_barrier((source, own[g]))
        stays = row // q == y
        turned = [lax.ppermute(own[g], ("row", "col"), turn) for g in range(groups)]
        gathered = {}
        flag = end.astype(jnp.int32).reshape(1)

        def gather(i):
            gathered[i] = [lax.ppermute(pieces[i], "col", along_x(s)) for s in range(1, nx)]

        for i in range(EARLY):
            gather(i)

        place = jnp.stack([row, y, x])
        factors = []
        parts = lambda i: [pieces[i]] + gathered[i]
        first = [[] for _ in range(1, ny)]
        for g in range(groups):
            held = jnp.where(stays, own[g], turned[g])
            blocks = [held] + [
                lax.ppermute(held, "row", [(r, (r + s) % rows) for r in range(rows)]) for s in range(1, rows)
            ]
            factors.append(arrange(place, blocks, nx, ny, depth))
            for t in range(1, ny):
                value = product([parts(0)], [[factors[g][t]]])[0][0]
                first[t - 1].append(lax.ppermute(value, "col", along_y(t)))
        near, sent = {}, {0: [jnp.concatenate(pair, axis=1) for pair in first]}

        def multiply(which):
            which = [i for i in which if i < n]
            if not which:
                return
            sets = [[group[t] for group in factors] for t in range(ny)]
            found = product([parts(i) for i in which], sets)
            for k, i in enumerate(which):
                near[i] = found[0][k]
                sent[i] = [lax.ppermute(found[t][k], "col", along_y(t)) for t in range(1, ny)]

        multiply(WORK[-2])
        near[0] = product([parts(0)], [[group[0] for group in factors]])[0][0]
        multiply(WORK[-1])
        starts = [unit * sum(SHARES[:i]) for i in range(n)]
        result = jnp.zeros((panels.shape[0], width), jnp.float32)
        total, summed, done, paired, crossed = {}, {}, {}, {}, {}
        for i in range(n + LAG + 2):
            multiply(WORK.get(i, ()))
            k = i - LAG
            if i < n and 0 <= k and SHARES[i] == SHARES[k]:
                total[i], done[k], give = combine(flag, [near[i], *sent[i]], [summed[k], crossed[k]])
                paired[i] = (lax.ppermute(give, "layer", pairs),) * 2
            else:
                paired[i] = [None, None]
                if i < n:
                    total[i] = combine(flag, [near[i], *sent[i]])[0]
                    paired[i][0] = lax.ppermute(total[i], "layer", pairs[0::3])
                if 0 <= k < n:
                    done[k] = combine(flag, [summed[k], crossed[k]])[0]
                    paired[i][1] = lax.ppermute(done[k], "layer", pairs[1:3])
            for late in LATE.get(i, ()):
                if late < n:
                    gather(late)
            k = i - 1
            if 0 <= k < n:
                summed[k] = combine(flag, [total[k], paired[k][0]])[0]
                crossed[k] = lax.ppermute(summed[k], "layer", across)
            k = i - LAG - 1
            if 0 <= k < n:
                value = jnp.where(end, paired[k + LAG][1], done[k])
                result = lax.dynamic_update_slice(result, value, (starts[k], 0))
        return result

    in_specs = (P("row", ("layer", "col")), P(("layer", "row"), "col"))
    out_specs = P("row", "col")
    step = jax.shard_map(body, mesh=mesh, in_specs=in_specs, out_specs=out_specs, check_vma=False)

    def traced(panels, eigvecs):
        jax.eval_shape(step, panels, eigvecs)
        return step(panels, eigvecs)

    return traced
```

time: 251 us -> 224 us (0.89)
  waiting for transfers between devices: 101 us -> 79.1 us
  other arithmetic: 14.7 us -> 5.26 us
  local copies, waits for them, and re-layouts: 9.54 us -> 15.3 us
  starting transfers between devices: 104 us -> 98.8 us
  Pallas kernels: 20.3 us -> 23.8 us
    ppermute x10, waiting for transfers between devices: 30.3 us -> 17.8 us  [gather(): lax.ppermute(pieces[i], 'col', along_x(s))]
    ppermute x22, waiting for transfers between devices: 66.6 us -> 61.3 us  [the longest x9 24.7 us: multiply(): lax.ppermute(found[t][k], 'col', along_y(t))]
    pallas_call x0 -> x25, Pallas kernels: none -> 5.33 us  [the longest x2 3.73 us: arrange(): pl.pallas_call(lambda *refs: arrange_kernel(nx, ny, depth, *refs), grid=(...]
    add x16 -> x0, other arithmetic: 4.36 us -> none  [add(): return a + b]
    ppermute x2, waiting for transfers between devices: 4.29 us -> 0.01 us  [body(): first[t - 1].append(lax.ppermute(value, 'col', along_y(t)))]
    convert_element_type x6 -> x0, other arithmetic: 3.83 us -> none  [arrange(): terms += [high.astype(jnp.bfloat16), (value - high).astype(jnp.bfloat16)]]
    unnamed x62 -> x76, local copies, waits for them, and re-layouts: 4.76 us -> 8.16 us
    ppermute x22, starting transfers between devices: 54.9 us -> 52.1 us  [the longest x7 29.4 us: body(): paired[i] = (lax.ppermute(give, 'layer', pairs),) * 2]
  transfers between devices with their start and end apart: 48 -> 48, of which waited for: 21 -> 15; matrix products, arithmetic and copies ran while one was open for 7% -> 5% of each run, Pallas kernels for 8% -> 11%
where the time goes in v2:
time: 224 us; the launch traced here: 223 us
  starting transfers between devices  98.8 us (44%)
  waiting for transfers between devices  79.1 us (35%)
  Pallas kernels  23.8 us (11%)
  local copies, waits for them, and re-layouts  15.3 us (7%)
  other arithmetic  5.26 us (2%)
    ppermute x7, starting transfers between devices, body(): paired[i] = (lax.ppermute(give, 'layer', pairs),) * 2  29.4 us
    ppermute x9, waiting for transfers between devices, multiply(): lax.ppermute(found[t][k], 'col', along_y(t))  24.7 us
    ppermute x2, starting transfers between devices, body(): lax.ppermute(held, 'row', [(r, (r + s) % rows) for r in range(rows)])  22.9 us
    ppermute x7, waiting for transfers between devices, body(): paired[i] = (lax.ppermute(give, 'layer', pairs),) * 2  18.4 us
    pallas_call x9, Pallas kernels, product(): pl.pallas_call(lambda *refs: product_kernel(len(pieces), nx, len(sets), g...  18.4 us
    ppermute x3, waiting for transfers between devices, body(): paired[i][1] = lax.ppermute(done[k], 'layer', pairs[1:3])  18.1 us
    ppermute x10, waiting for transfers between devices, gather(): lax.ppermute(pieces[i], 'col', along_x(s))  17.8 us
    ppermute x9, starting transfers between devices, multiply(): lax.ppermute(found[t][k], 'col', along_y(t))  12.4 us
  transfers between devices with their start and end apart: 48, of which 15 were waited for; matrix products, arithmetic and copies ran while one was open for 5% of the time, Pallas kernels for 11%

profile of v2, /device:TPU:0, one launch (start us, length us, event | category | flops | bytes accessed | tf_op | source)
XLA Modules:
  0.0 223.0 jit_solution(3264541260615395029)
XLA Ops:
  7.3 13.1 %collective-permute-start.2 = (f32[1024,256]{1,0:T(8,128)S(1)}, f32[1024,256]{1,0:T(8,128)}, u32[]{:S(2)}, u32[]{:S(2)}) collective-permute-start(f32[1024,256]{1,0:T(8,128)S(1)} %broadcast_select_fusion.1.refs_1_), channel_id=1, source_target_pairs={{0,4},{4,0},{1,5},{5,1},{2,6},{6,2},{3,7},{7,3},{8,12},{12,8},{9,1... | collective-permute-start | bytes 3145736 | tf_op jit(solution)/shard_map/ppermute | solution.py:192
  21.7 9.9 %collective-permute-start.4 = (f32[1024,256]{1,0:T(8,128)S(1)}, f32[1024,256]{1,0:T(8,128)}, u32[]{:S(2)}, u32[]{:S(2)}) collective-permute-start(f32[1024,256]{1,0:T(8,128)S(1)} %broadcast_select_fusion.refs_1_), channel_id=1, source_target_pairs={{0,4},{4,0},{1,5},{5,1},{2,6},{6,2},{3,7},{7,3},{8,12},{12,8},{9,1... | collective-permute-start | bytes 3145736 | tf_op jit(solution)/shard_map/ppermute | solution.py:192
  31.6 2.5 %fusion = (f32[224,512]{1,0:T(8,128)}, f32[224,512]{1,0:T(8,128)}, f32[224,512]{1,0:T(8,128)S(1)}, f32[224,512]{1,0:T(8,128)}) fusion(f32[2048,512]{1,0:T(8,128)} %param.2), kind=kLoop, calls=%fused_computation.14 | loop fusion | bytes 3670016 | tf_op jit(solution)/shard_map/slice | solution.py:166
  36.2 1.9 arrange.2
  38.9 8.6 %collective-permute-done.6.refs_1_ = f32[224,512]{1,0:T(8,128)S(1)} collective-permute-done((f32[224,512]{1,0:T(8,128)S(1)}, f32[224,512]{1,0:T(8,128)S(1)}, u32[]{:S(2)}, u32[]{:S(2)}) %collective-permute-start.6) | collective-permute-done | bytes 458784 | tf_op jit(solution)/shard_map/ppermute | solution.py:180
  66.4 3.5 %collective-permute-start.9 = (f32[224,512]{1,0:T(8,128)S(1)}, f32[224,512]{1,0:T(8,128)S(1)}, u32[]{:S(2)}, u32[]{:S(2)}) collective-permute-start(f32[224,512]{1,0:T(8,128)S(1)} %combine.23.refs_1_), channel_id=1, source_target_pairs={{0,8},{24,16},{1,9},{25,17},{2,10},{26,18},{3,11},{27,19},{4,12},{... | collective-permute-start | bytes 1376264 | tf_op jit(solution)/shard_map/ppermute | solution.py:226
  70.6 2.5 %product.15 = (f32[192,512]{1,0:T(8,128)S(1)}, f32[192,512]{1,0:T(8,128)S(1)}) custom-call(f32[192,512]{1,0:T(8,128)} %get-tuple-element.125.refs_0_, f32[192,512]{1,0:T(8,128)} %collective-permute-done.21.refs_1_, bf16[512,256]{1,0:T(8,128)(2,1)S(1)} %copy-done.6, bf16[512,256]{1,0:T(8,128)(2,1)S(1)} %copy-done.8, bf16[512,256]{1,0:T(8,128)(2,1)S(1)} %copy-done.11, ...), custom_call_target="tpu_custom_call" | custom-call | flops 1207959552 | bytes 393216 | tf_op jit(solution)/shard_map/product/pallas_call | solution.py:53
  74.8 2.8 %product.9 = (f32[224,512]{1,0:T(8,128)S(1)}, f32[224,512]{1,0:T(8,128)S(1)}) custom-call(f32[224,512]{1,0:T(8,128)} %get-tuple-element.122.refs_0_, f32[224,512]{1,0:T(8,128)} %collective-permute-done.refs_1_, bf16[512,256]{1,0:T(8,128)(2,1)S(1)} %copy-done.6, bf16[512,256]{1,0:T(8,128)(2,1)S(1)} %copy-done.8, bf16[512,256]{1,0:T(8,128)(2,1)S(1)} %copy-done.11, ...), custom_call_target="tpu_custom_call" | custom-call | flops 1409286144 | bytes 458752 | tf_op jit(solution)/shard_map/product/pallas_call | solution.py:53
  86.7 13.5 %collective-permute-done.16.refs_2_ = f32[192,512]{1,0:T(8,128)S(1)} collective-permute-done((f32[192,512]{1,0:T(8,128)S(1)}, f32[192,512]{1,0:T(8,128)S(1)}, u32[]{:S(2)}, u32[]{:S(2)}) %collective-permute-start.16) | collective-permute-done | bytes 393248 | tf_op jit(solution)/shard_map/ppermute | solution.py:208
  105.3 2.5 %collective-permute-start.11 = (f32[224,512]{1,0:T(8,128)S(1)}, f32[224,512]{1,0:T(8,128)S(1)}, u32[]{:S(2)}, u32[]{:S(2)}) collective-permute-start(f32[224,512]{1,0:T(8,128)S(1)} %get-tuple-element.82), channel_id=1, source_target_pairs={{0,8},{8,0},{16,24},{24,16},{1,9},{9,1},{17,25},{25,17},{2,10},{10... | collective-permute-start | bytes 1376264 | tf_op jit(solution)/shard_map/ppermute | solution.py:221
  107.8 2.6 %product.13 = (f32[192,512]{1,0:T(8,128)S(1)}, f32[192,512]{1,0:T(8,128)S(1)}, f32[192,512]{1,0:T(8,128)S(1)}, f32[192,512]{1,0:T(8,128)S(1)}) custom-call(f32[192,512]{1,0:T(8,128)S(1)} %copy-done.33, f32[192,512]{1,0:T(8,128)S(1)} %collective-permute-done.12.refs_1_, f32[192,512]{1,0:T(8,128)S(1)} %copy-done.32, ...), custom_call_target="tpu_custom_call" | custom-call | flops 2415919104 | bytes 786432 | tf_op jit(solution)/shard_map/product/pallas_call | solution.py:53
  110.5 7.3 %collective-permute-done.27.refs_3_ = f32[192,512]{1,0:T(8,128)S(1)} collective-permute-done((f32[192,512]{1,0:T(8,128)S(1)}, f32[192,512]{1,0:T(8,128)S(1)}, u32[]{:S(2)}, u32[]{:S(2)}) %collective-permute-start.27) | collective-permute-done | bytes 393248 | tf_op jit(solution)/shard_map/ppermute | solution.py:180
  120.9 2.9 %product.16 = (f32[224,512]{1,0:T(8,128)S(1)}, f32[192,512]{1,0:T(8,128)S(1)}, f32[224,512]{1,0:T(8,128)S(1)}, f32[192,512]{1,0:T(8,128)S(1)}) custom-call(f32[224,512]{1,0:T(8,128)S(1)} %copy-done.29, f32[224,512]{1,0:T(8,128)S(1)} %collective-permute-done.26.refs_1_, f32[192,512]{1,0:T(8,128)S(1)} %copy-done.31, ...), custom_call_target="tpu_custom_call" | custom-call | flops 2617245696 | bytes 851968 | tf_op jit(solution)/shard_map/product/pallas_call | solution.py:53
  123.8 1.9 collective-permute-start.28
  127.8 2.0 collective-permute-done.14.refs_2_
  130.5 7.7 %collective-permute-done.20.refs_2_ = f32[192,512]{1,0:T(8,128)S(1)} collective-permute-done((f32[192,512]{1,0:T(8,128)S(1)}, f32[192,512]{1,0:T(8,128)S(1)}, u32[]{:S(2)}, u32[]{:S(2)}) %collective-permute-start.20) | collective-permute-done | bytes 393248 | tf_op jit(solution)/shard_map/ppermute | solution.py:208
  140.4 4.3 %collective-permute-start.19 = (f32[192,512]{1,0:T(8,128)S(1)}, f32[192,512]{1,0:T(8,128)S(1)}, u32[]{:S(2)}, u32[]{:S(2)}) collective-permute-start(f32[192,512]{1,0:T(8,128)S(1)} %get-tuple-element.88), channel_id=1, source_target_pairs={{0,8},{8,0},{16,24},{24,16},{1,9},{9,1},{17,25},{25,17},{2,10},{10... | collective-permute-start | bytes 1179656 | tf_op jit(solution)/shard_map/ppermute | solution.py:221
  144.8 2.5 %collective-permute-start.25 = (f32[192,512]{1,0:T(8,128)S(1)}, f32[192,512]{1,0:T(8,128)S(1)}, u32[]{:S(2)}, u32[]{:S(2)}) collective-permute-start(f32[192,512]{1,0:T(8,128)S(1)} %get-tuple-element.94), channel_id=1, source_target_pairs={{0,8},{8,0},{16,24},{24,16},{1,9},{9,1},{17,25},{25,17},{2,10},{10... | collective-permute-start | bytes 1179656 | tf_op jit(solution)/shard_map/ppermute | solution.py:221
  149.0 1.9 collective-permute-done.34.refs_1_
  150.9 4.2 %collective-permute-start.30 = (f32[224,512]{1,0:T(8,128)S(1)}, f32[224,512]{1,0:T(8,128)S(1)}, u32[]{:S(2)}, u32[]{:S(2)}) collective-permute-start(f32[224,512]{1,0:T(8,128)S(1)} %get-tuple-element.99), channel_id=1, source_target_pairs={{0,8},{8,0},{16,24},{24,16},{1,9},{9,1},{17,25},{25,17},{2,10},{10... | collective-permute-start | bytes 1376264 | tf_op jit(solution)/shard_map/ppermute | solution.py:221
  155.1 2.8 %product.17 = (f32[192,512]{1,0:T(8,128)S(1)}, f32[224,512]{1,0:T(8,128)S(1)}, f32[192,512]{1,0:T(8,128)S(1)}, f32[224,512]{1,0:T(8,128)S(1)}) custom-call(f32[192,512]{1,0:T(8,128)S(1)} %copy-done.30, f32[192,512]{1,0:T(8,128)S(1)} %collective-permute-done.34.refs_1_, f32[224,512]{1,0:T(8,128)S(1)} %copy-done.28, ...), custom_call_target="tpu_custom_call" | custom-call | flops 2617245696 | bytes 851968 | tf_op jit(solution)/shard_map/product/pallas_call | solution.py:53
  158.7 2.0 collective-permute-start.36
  160.7 2.0 collective-permute-done.25.refs_2_
  165.2 5.3 %collective-permute-start.33 = (f32[192,512]{1,0:T(8,128)S(1)}, f32[192,512]{1,0:T(8,128)S(1)}, u32[]{:S(2)}, u32[]{:S(2)}) collective-permute-start(f32[192,512]{1,0:T(8,128)S(1)} %get-tuple-element.104), channel_id=1, source_target_pairs={{0,8},{8,0},{16,24},{24,16},{1,9},{9,1},{17,25},{25,17},{2,10},{10... | collective-permute-start | bytes 1179656 | tf_op jit(solution)/shard_map/ppermute | solution.py:221
  170.6 5.0 %collective-permute-start.38 = (f32[192,512]{1,0:T(8,128)S(1)}, f32[192,512]{1,0:T(8,128)S(1)}, u32[]{:S(2)}, u32[]{:S(2)}) collective-permute-start(f32[192,512]{1,0:T(8,128)S(1)} %get-tuple-element.109), channel_id=1, source_target_pairs={{0,8},{8,0},{16,24},{24,16},{1,9},{9,1},{17,25},{25,17},{2,10},{10... | collective-permute-start | bytes 1179656 | tf_op jit(solution)/shard_map/ppermute | solution.py:221
  176.5 3.8 %collective-permute-done.33.refs_2_ = f32[192,512]{1,0:T(8,128)S(1)} collective-permute-done((f32[192,512]{1,0:T(8,128)S(1)}, f32[192,512]{1,0:T(8,128)S(1)}, u32[]{:S(2)}, u32[]{:S(2)}) %collective-permute-start.33) | collective-permute-done | bytes 393248 | tf_op jit(solution)/shard_map/ppermute | solution.py:221
  181.0 3.5 %collective-permute-done.38.refs_2_ = f32[192,512]{1,0:T(8,128)S(1)} collective-permute-done((f32[192,512]{1,0:T(8,128)S(1)}, f32[192,512]{1,0:T(8,128)S(1)}, u32[]{:S(2)}, u32[]{:S(2)}) %collective-permute-start.38) | collective-permute-done | bytes 393248 | tf_op jit(solution)/shard_map/ppermute | solution.py:221
  185.4 5.6 %collective-permute-start.41 = (f32[224,512]{1,0:T(8,128)S(1)}, f32[224,512]{1,0:T(8,128)S(1)}, u32[]{:S(2)}, u32[]{:S(2)}) collective-permute-start(f32[224,512]{1,0:T(8,128)S(1)} %get-tuple-element.114), channel_id=1, source_target_pairs={{0,8},{8,0},{16,24},{24,16},{1,9},{9,1},{17,25},{25,17},{2,10},{10... | collective-permute-start | bytes 1376264 | tf_op jit(solution)/shard_map/ppermute | solution.py:221
  192.5 7.8 %collective-permute-done.41.refs_2_ = f32[224,512]{1,0:T(8,128)S(1)} collective-permute-done((f32[224,512]{1,0:T(8,128)S(1)}, f32[224,512]{1,0:T(8,128)S(1)}, u32[]{:S(2)}, u32[]{:S(2)}) %collective-permute-start.41) | collective-permute-done | bytes 458784 | tf_op jit(solution)/shard_map/ppermute | solution.py:221
  204.0 3.2 %collective-permute-done.43 = f32[192,512]{1,0:T(8,128)S(1)} collective-permute-done((f32[192,512]{1,0:T(8,128)S(1)}, f32[192,512]{1,0:T(8,128)S(1)}, u32[]{:S(2)}, u32[]{:S(2)}) %collective-permute-start.43) | collective-permute-done | bytes 393248 | tf_op jit(solution)/shard_map/ppermute | solution.py:229
  207.2 10.0 %collective-permute-done.45 = f32[192,512]{1,0:T(8,128)S(1)} collective-permute-done((f32[192,512]{1,0:T(8,128)S(1)}, f32[192,512]{1,0:T(8,128)S(1)}, u32[]{:S(2)}, u32[]{:S(2)}) %collective-permute-start.45) | collective-permute-done | bytes 393248 | tf_op jit(solution)/shard_map/ppermute | solution.py:229
  217.4 4.8 %collective-permute-done.47 = f32[224,512]{1,0:T(8,128)S(1)} collective-permute-done((f32[224,512]{1,0:T(8,128)S(1)}, f32[224,512]{1,0:T(8,128)S(1)}, u32[]{:S(2)}, u32[]{:S(2)}) %collective-permute-start.47) | collective-permute-done | bytes 458784 | tf_op jit(solution)/shard_map/ppermute | solution.py:229
  (193 shorter events, 68.3 us)
Async XLA Ops:
  4.3 16.1 %collective-permute-start.3 = (f32[1024,256]{1,0:T(8,128)S(1)}, f32[1024,256]{1,0:T(8,128)}, u32[]{:S(2)}, u32[]{:S(2)}) collective-permute-start(f32[1024,256]{1,0:T(8,128)S(1)} %slice.38), channel_id=1, source_target_pairs={{2,4},{3,5},{4,2},{5,3},{10,12},{11,13},{12,10},{13,11},{18,20},{1... | collective-permute-start | bytes 3145736 | tf_op jit(solution)/shard_map/ppermute | solution.py:175
  7.3 28.9 %collective-permute-start.2 = (f32[1024,256]{1,0:T(8,128)S(1)}, f32[1024,256]{1,0:T(8,128)}, u32[]{:S(2)}, u32[]{:S(2)}) collective-permute-start(f32[1024,256]{1,0:T(8,128)S(1)} %broadcast_select_fusion.1.refs_1_), channel_id=1, source_target_pairs={{0,4},{4,0},{1,5},{5,1},{2,6},{6,2},{3,7},{7,3},{8,12},{12,8},{9,1... | collective-permute-start | bytes 3145736 | tf_op jit(solution)/shard_map/ppermute | solution.py:192
  21.7 28.7 %collective-permute-start.4 = (f32[1024,256]{1,0:T(8,128)S(1)}, f32[1024,256]{1,0:T(8,128)}, u32[]{:S(2)}, u32[]{:S(2)}) collective-permute-start(f32[1024,256]{1,0:T(8,128)S(1)} %broadcast_select_fusion.refs_1_), channel_id=1, source_target_pairs={{0,4},{4,0},{1,5},{5,1},{2,6},{6,2},{3,7},{7,3},{8,12},{12,8},{9,1... | collective-permute-start | bytes 3145736 | tf_op jit(solution)/shard_map/ppermute | solution.py:192
  35.6 39.2 %collective-permute-start = (f32[224,512]{1,0:T(8,128)}, f32[224,512]{1,0:T(8,128)}, u32[]{:S(2)}, u32[]{:S(2)}) collective-permute-start(f32[224,512]{1,0:T(8,128)} %get-tuple-element.122.refs_0_), channel_id=1, source_target_pairs={{0,1},{1,0},{2,3},{3,2},{4,5},{5,4},{6,7},{7,6},{8,9},{9,8},{10,11... | collective-permute-start | bytes 1376264 | tf_op jit(solution)/shard_map/ppermute | solution.py:180
  48.8 16.4 %collective-permute-start.7 = (f32[224,256]{1,0:T(8,128)}, f32[224,256]{1,0:T(8,128)}, u32[]{:S(2)}, u32[]{:S(2)}) collective-permute-start(f32[224,256]{1,0:T(8,128)} %product.11), channel_id=1, source_target_pairs={{0,2},{1,3},{2,0},{3,1},{4,6},{5,7},{6,4},{7,5},{8,10},{9,11},{10,... | collective-permute-start | bytes 688136 | tf_op jit(solution)/shard_map/ppermute | solution.py:197
  56.1 14.4 %collective-permute-start.21 = (f32[192,512]{1,0:T(8,128)}, f32[192,512]{1,0:T(8,128)}, u32[]{:S(2)}, u32[]{:S(2)}) collective-permute-start(f32[192,512]{1,0:T(8,128)} %get-tuple-element.125.refs_0_), channel_id=1, source_target_pairs={{0,1},{1,0},{2,3},{3,2},{4,5},{5,4},{6,7},{7,6},{8,9},{9,8},{10,11... | collective-permute-start | bytes 1179656 | tf_op jit(solution)/shard_map/ppermute | solution.py:180
  77.6 24.0 %collective-permute-start.5 = (f32[224,512]{1,0:T(8,128)S(1)}, f32[224,512]{1,0:T(8,128)S(1)}, u32[]{:S(2)}, u32[]{:S(2)}) collective-permute-start(f32[224,512]{1,0:T(8,128)S(1)} %get-tuple-element.81), channel_id=1, source_target_pairs={{0,2},{1,3},{2,0},{3,1},{4,6},{5,7},{6,4},{7,5},{8,10},{9,11},{10,... | collective-permute-start | bytes 1376264 | tf_op jit(solution)/shard_map/ppermute | solution.py:208
  78.2 24.1 %collective-permute-start.10 = (f32[224,512]{1,0:T(8,128)S(1)}, f32[224,512]{1,0:T(8,128)S(1)}, u32[]{:S(2)}, u32[]{:S(2)}) collective-permute-start(f32[224,512]{1,0:T(8,128)S(1)} %combine.24.refs_3_), channel_id=1, source_target_pairs={{8,16},{16,8},{9,17},{17,9},{10,18},{18,10},{11,19},{19,11},{12,20... | collective-permute-start | bytes 1376264 | tf_op jit(solution)/shard_map/ppermute | solution.py:236
  80.4 19.7 %collective-permute-start.16 = (f32[192,512]{1,0:T(8,128)S(1)}, f32[192,512]{1,0:T(8,128)S(1)}, u32[]{:S(2)}, u32[]{:S(2)}) collective-permute-start(f32[192,512]{1,0:T(8,128)S(1)} %get-tuple-element.87), channel_id=1, source_target_pairs={{0,2},{1,3},{2,0},{3,1},{4,6},{5,7},{6,4},{7,5},{8,10},{9,11},{10,... | collective-permute-start | bytes 1179656 | tf_op jit(solution)/shard_map/ppermute | solution.py:208
  82.1 21.9 %collective-permute-start.13 = (f32[192,512]{1,0:T(8,128)S(1)}, f32[192,512]{1,0:T(8,128)S(1)}, u32[]{:S(2)}, u32[]{:S(2)}) collective-permute-start(f32[192,512]{1,0:T(8,128)S(1)} %copy-done.32), channel_id=1, source_target_pairs={{0,1},{1,0},{2,3},{3,2},{4,5},{5,4},{6,7},{7,6},{8,9},{9,8},{10,11... | collective-permute-start | bytes 1179656 | tf_op jit(solution)/shard_map/ppermute | solution.py:180
  85.2 20.1 %collective-permute-start.12 = (f32[192,512]{1,0:T(8,128)S(1)}, f32[192,512]{1,0:T(8,128)S(1)}, u32[]{:S(2)}, u32[]{:S(2)}) collective-permute-start(f32[192,512]{1,0:T(8,128)S(1)} %copy-done.33), channel_id=1, source_target_pairs={{0,1},{1,0},{2,3},{3,2},{4,5},{5,4},{6,7},{7,6},{8,9},{9,8},{10,11... | collective-permute-start | bytes 1179656 | tf_op jit(solution)/shard_map/ppermute | solution.py:180
  100.1 19.8 %collective-permute-start.26 = (f32[224,512]{1,0:T(8,128)S(1)}, f32[224,512]{1,0:T(8,128)S(1)}, u32[]{:S(2)}, u32[]{:S(2)}) collective-permute-start(f32[224,512]{1,0:T(8,128)S(1)} %copy-done.29), channel_id=1, source_target_pairs={{0,1},{1,0},{2,3},{3,2},{4,5},{5,4},{6,7},{7,6},{8,9},{9,8},{10,11... | collective-permute-start | bytes 1376264 | tf_op jit(solution)/shard_map/ppermute | solution.py:180
  101.6 16.2 %collective-permute-start.27 = (f32[192,512]{1,0:T(8,128)S(1)}, f32[192,512]{1,0:T(8,128)S(1)}, u32[]{:S(2)}, u32[]{:S(2)}) collective-permute-start(f32[192,512]{1,0:T(8,128)S(1)} %copy-done.31), channel_id=1, source_target_pairs={{0,1},{1,0},{2,3},{3,2},{4,5},{5,4},{6,7},{7,6},{8,9},{9,8},{10,11... | collective-permute-start | bytes 1179656 | tf_op jit(solution)/shard_map/ppermute | solution.py:180
  102.2 17.4 %collective-permute-start.17 = (f32[192,512]{1,0:T(8,128)S(1)}, f32[192,512]{1,0:T(8,128)S(1)}, u32[]{:S(2)}, u32[]{:S(2)}) collective-permute-start(f32[192,512]{1,0:T(8,128)S(1)} %combine.26.refs_1_), channel_id=1, source_target_pairs={{0,8},{24,16},{1,9},{25,17},{2,10},{26,18},{3,11},{27,19},{4,12},{... | collective-permute-start | bytes 1179656 | tf_op jit(solution)/shard_map/ppermute | solution.py:226
  104.0 19.8 %collective-permute-start.23 = (f32[192,512]{1,0:T(8,128)S(1)}, f32[192,512]{1,0:T(8,128)S(1)}, u32[]{:S(2)}, u32[]{:S(2)}) collective-permute-start(f32[192,512]{1,0:T(8,128)S(1)} %combine.29.refs_1_), channel_id=1, source_target_pairs={{0,8},{24,16},{1,9},{25,17},{2,10},{26,18},{3,11},{27,19},{4,12},{... | collective-permute-start | bytes 1179656 | tf_op jit(solution)/shard_map/ppermute | solution.py:226
  105.3 21.7 %collective-permute-start.11 = (f32[224,512]{1,0:T(8,128)S(1)}, f32[224,512]{1,0:T(8,128)S(1)}, u32[]{:S(2)}, u32[]{:S(2)}) collective-permute-start(f32[224,512]{1,0:T(8,128)S(1)} %get-tuple-element.82), channel_id=1, source_target_pairs={{0,8},{8,0},{16,24},{24,16},{1,9},{9,1},{17,25},{25,17},{2,10},{10... | collective-permute-start | bytes 1376264 | tf_op jit(solution)/shard_map/ppermute | solution.py:221
  119.6 18.6 %collective-permute-start.20 = (f32[192,512]{1,0:T(8,128)S(1)}, f32[192,512]{1,0:T(8,128)S(1)}, u32[]{:S(2)}, u32[]{:S(2)}) collective-permute-start(f32[192,512]{1,0:T(8,128)S(1)} %get-tuple-element.91), channel_id=1, source_target_pairs={{0,2},{1,3},{2,0},{3,1},{4,6},{5,7},{6,4},{7,5},{8,10},{9,11},{10,... | collective-permute-start | bytes 1179656 | tf_op jit(solution)/shard_map/ppermute | solution.py:208
  119.9 19.8 %collective-permute-start.18 = (f32[192,512]{1,0:T(8,128)S(1)}, f32[192,512]{1,0:T(8,128)S(1)}, u32[]{:S(2)}, u32[]{:S(2)}) collective-permute-start(f32[192,512]{1,0:T(8,128)S(1)} %combine.27.refs_3_), channel_id=1, source_target_pairs={{8,16},{16,8},{9,17},{17,9},{10,18},{18,10},{11,19},{19,11},{12,20... | collective-permute-start | bytes 1179656 | tf_op jit(solution)/shard_map/ppermute | solution.py:236
  123.8 21.0 %collective-permute-start.28 = (f32[224,512]{1,0:T(8,128)S(1)}, f32[224,512]{1,0:T(8,128)S(1)}, u32[]{:S(2)}, u32[]{:S(2)}) collective-permute-start(f32[224,512]{1,0:T(8,128)S(1)} %get-tuple-element.97), channel_id=1, source_target_pairs={{0,2},{1,3},{2,0},{3,1},{4,6},{5,7},{6,4},{7,5},{8,10},{9,11},{10,... | collective-permute-start | bytes 1376264 | tf_op jit(solution)/shard_map/ppermute | solution.py:208
  129.8 17.5 %collective-permute-start.29 = (f32[224,512]{1,0:T(8,128)S(1)}, f32[224,512]{1,0:T(8,128)S(1)}, u32[]{:S(2)}, u32[]{:S(2)}) collective-permute-start(f32[224,512]{1,0:T(8,128)S(1)} %combine.32.refs_3_), channel_id=1, source_target_pairs={{8,16},{16,8},{9,17},{17,9},{10,18},{18,10},{11,19},{19,11},{12,20... | collective-permute-start | bytes 1376264 | tf_op jit(solution)/shard_map/ppermute | solution.py:236
  138.2 16.9 %collective-permute-start.35 = (f32[224,512]{1,0:T(8,128)S(1)}, f32[224,512]{1,0:T(8,128)S(1)}, u32[]{:S(2)}, u32[]{:S(2)}) collective-permute-start(f32[224,512]{1,0:T(8,128)S(1)} %copy-done.28), channel_id=1, source_target_pairs={{0,1},{1,0},{2,3},{3,2},{4,5},{5,4},{6,7},{7,6},{8,9},{9,8},{10,11... | collective-permute-start | bytes 1376264 | tf_op jit(solution)/shard_map/ppermute | solution.py:180
  140.4 17.6 %collective-permute-start.19 = (f32[192,512]{1,0:T(8,128)S(1)}, f32[192,512]{1,0:T(8,128)S(1)}, u32[]{:S(2)}, u32[]{:S(2)}) collective-permute-start(f32[192,512]{1,0:T(8,128)S(1)} %get-tuple-element.88), channel_id=1, source_target_pairs={{0,8},{8,0},{16,24},{24,16},{1,9},{9,1},{17,25},{25,17},{2,10},{10... | collective-permute-start | bytes 1179656 | tf_op jit(solution)/shard_map/ppermute | solution.py:221
  144.8 17.9 %collective-permute-start.25 = (f32[192,512]{1,0:T(8,128)S(1)}, f32[192,512]{1,0:T(8,128)S(1)}, u32[]{:S(2)}, u32[]{:S(2)}) collective-permute-start(f32[192,512]{1,0:T(8,128)S(1)} %get-tuple-element.94), channel_id=1, source_target_pairs={{0,8},{8,0},{16,24},{24,16},{1,9},{9,1},{17,25},{25,17},{2,10},{10... | collective-permute-start | bytes 1179656 | tf_op jit(solution)/shard_map/ppermute | solution.py:221
  147.3 16.8 %collective-permute-start.31 = (f32[192,512]{1,0:T(8,128)S(1)}, f32[192,512]{1,0:T(8,128)S(1)}, u32[]{:S(2)}, u32[]{:S(2)}) collective-permute-start(f32[192,512]{1,0:T(8,128)S(1)} %get-tuple-element.102), channel_id=1, source_target_pairs={{0,2},{1,3},{2,0},{3,1},{4,6},{5,7},{6,4},{7,5},{8,10},{9,11},{10,... | collective-permute-start | bytes 1179656 | tf_op jit(solution)/shard_map/ppermute | solution.py:208
  150.9 24.7 %collective-permute-start.30 = (f32[224,512]{1,0:T(8,128)S(1)}, f32[224,512]{1,0:T(8,128)S(1)}, u32[]{:S(2)}, u32[]{:S(2)}) collective-permute-start(f32[224,512]{1,0:T(8,128)S(1)} %get-tuple-element.99), channel_id=1, source_target_pairs={{0,8},{8,0},{16,24},{24,16},{1,9},{9,1},{17,25},{25,17},{2,10},{10... | collective-permute-start | bytes 1376264 | tf_op jit(solution)/shard_map/ppermute | solution.py:221
  164.1 21.1 %collective-permute-start.39 = (f32[224,512]{1,0:T(8,128)S(1)}, f32[224,512]{1,0:T(8,128)S(1)}, u32[]{:S(2)}, u32[]{:S(2)}) collective-permute-start(f32[224,512]{1,0:T(8,128)S(1)} %get-tuple-element.112), channel_id=1, source_target_pairs={{0,2},{1,3},{2,0},{3,1},{4,6},{5,7},{6,4},{7,5},{8,10},{9,11},{10,... | collective-permute-start | bytes 1376264 | tf_op jit(solution)/shard_map/ppermute | solution.py:208
  165.2 15.0 %collective-permute-start.33 = (f32[192,512]{1,0:T(8,128)S(1)}, f32[192,512]{1,0:T(8,128)S(1)}, u32[]{:S(2)}, u32[]{:S(2)}) collective-permute-start(f32[192,512]{1,0:T(8,128)S(1)} %get-tuple-element.104), channel_id=1, source_target_pairs={{0,8},{8,0},{16,24},{24,16},{1,9},{9,1},{17,25},{25,17},{2,10},{10... | collective-permute-start | bytes 1179656 | tf_op jit(solution)/shard_map/ppermute | solution.py:221
  184.5 16.6 %collective-permute-start.44 = (f32[192,512]{1,0:T(8,128)S(1)}, f32[192,512]{1,0:T(8,128)S(1)}, u32[]{:S(2)}, u32[]{:S(2)}) collective-permute-start(f32[192,512]{1,0:T(8,128)S(1)} %combine.42.refs_1_), channel_id=1, source_target_pairs={{8,16},{16,8},{9,17},{17,9},{10,18},{18,10},{11,19},{19,11},{12,20... | collective-permute-start | bytes 1179656 | tf_op jit(solution)/shard_map/ppermute | solution.py:236
  185.4 15.0 %collective-permute-start.41 = (f32[224,512]{1,0:T(8,128)S(1)}, f32[224,512]{1,0:T(8,128)S(1)}, u32[]{:S(2)}, u32[]{:S(2)}) collective-permute-start(f32[224,512]{1,0:T(8,128)S(1)} %get-tuple-element.114), channel_id=1, source_target_pairs={{0,8},{8,0},{16,24},{24,16},{1,9},{9,1},{17,25},{25,17},{2,10},{10... | collective-permute-start | bytes 1376264 | tf_op jit(solution)/shard_map/ppermute | solution.py:221
  191.2 16.0 %collective-permute-start.43 = (f32[192,512]{1,0:T(8,128)S(1)}, f32[192,512]{1,0:T(8,128)S(1)}, u32[]{:S(2)}, u32[]{:S(2)}) collective-permute-start(f32[192,512]{1,0:T(8,128)S(1)} %combine.41), channel_id=1, source_target_pairs={{8,0},{16,24},{9,1},{17,25},{10,2},{18,26},{11,3},{19,27},{12,4},{... | collective-permute-start | bytes 1179656 | tf_op jit(solution)/shard_map/ppermute | solution.py:229
  201.2 16.1 %collective-permute-start.45 = (f32[192,512]{1,0:T(8,128)S(1)}, f32[192,512]{1,0:T(8,128)S(1)}, u32[]{:S(2)}, u32[]{:S(2)}) collective-permute-start(f32[192,512]{1,0:T(8,128)S(1)} %combine.43), channel_id=1, source_target_pairs={{8,0},{16,24},{9,1},{17,25},{10,2},{18,26},{11,3},{19,27},{12,4},{... | collective-permute-start | bytes 1179656 | tf_op jit(solution)/shard_map/ppermute | solution.py:229
  202.7 19.5 %collective-permute-start.47 = (f32[224,512]{1,0:T(8,128)S(1)}, f32[224,512]{1,0:T(8,128)S(1)}, u32[]{:S(2)}, u32[]{:S(2)}) collective-permute-start(f32[224,512]{1,0:T(8,128)S(1)} %combine.45), channel_id=1, source_target_pairs={{8,0},{16,24},{9,1},{17,25},{10,2},{18,26},{11,3},{19,27},{12,4},{... | collective-permute-start | bytes 1376264 | tf_op jit(solution)/shard_map/ppermute | solution.py:229
  (54 other events, 498.9 us)

commit v3 on v2

--- a/solution.py
+++ b/solution.py
@@ -6,11 +6,11 @@
 from jax.sharding import PartitionSpec as P
 
 
-SHARES = (7, 6, 6, 7, 6, 6, 7, 6, 6, 7)
+SHARES = (6, 6, 6, 6, 6, 6, 6, 6, 6, 6, 4)
 LAG = 3
 EARLY = 5
-LATE = {0: (5, 6), 1: (7,), 2: (8, 9, 10)}
-WORK = {-2: (1,), -1: (2,), 1: (3,), 3: (4, 5), 5: (6, 7), 7: (8, 9), 8: (10,)}
+LATE = {0: (5, 6), 1: (7, 8), 2: (9, 10)}
+WORK = {-2: (1,), -1: (2,), 1: (3,), 2: (4,), 3: (5,), 4: (6,), 5: (7,), 6: (8,), 7: (9,), 8: (10,)}
 VMEM = 12 * 2**20
 
 

time: 224 us -> 223 us (level)
  local copies, waits for them, and re-layouts: 15.3 us -> 7.8 us
  starting transfers between devices: 98.8 us -> 103 us
  waiting for transfers between devices: 79.1 us -> 83.3 us
    ppermute x10 -> x11, waiting for transfers between devices: 17.8 us -> 27.8 us  [gather(): lax.ppermute(pieces[i], 'col', along_x(s))]
    ppermute x9 -> x10, waiting for transfers between devices: 24.7 us -> 16.7 us  [multiply(): lax.ppermute(found[t][k], 'col', along_y(t))]
    ppermute x3 -> x4, waiting for transfers between devices: 0.01 us -> 7.47 us  [body(): paired[i][0] = lax.ppermute(total[i], 'layer', pairs[0::3])]
    unnamed x76 -> x20, local copies, waits for them, and re-layouts: 8.16 us -> 2.04 us
    ppermute x7, waiting for transfers between devices: 18.4 us -> 14 us  [body(): paired[i] = (lax.ppermute(give, 'layer', pairs),) * 2]
    ppermute x3 -> x4, starting transfers between devices: 6.4 us -> 10.4 us  [body(): paired[i][0] = lax.ppermute(total[i], 'layer', pairs[0::3])]
    ppermute x7, starting transfers between devices: 29.4 us -> 26.1 us  [body(): paired[i] = (lax.ppermute(give, 'layer', pairs),) * 2]
    ppermute x3 -> x4, starting transfers between devices: 3.88 us -> 5.16 us  [body(): paired[i][1] = lax.ppermute(done[k], 'layer', pairs[1:3])]
  transfers between devices with their start and end apart: 48 -> 53, of which waited for: 15 -> 18; matrix products, arithmetic and copies ran while one was open for 5% -> 4% of each run, Pallas kernels for 11% -> 10%
where the time goes in v3:
time: 223 us; the launch traced here: 222 us
  starting transfers between devices  103 us (46%)
  waiting for transfers between devices  83.3 us (37%)
  Pallas kernels  22.7 us (10%)
  local copies, waits for them, and re-layouts  7.8 us (3%)
  other arithmetic  4.28 us (2%)
    ppermute x11, waiting for transfers between devices, gather(): lax.ppermute(pieces[i], 'col', along_x(s))  27.8 us
    ppermute x7, starting transfers between devices, body(): paired[i] = (lax.ppermute(give, 'layer', pairs),) * 2  26.1 us
    ppermute x2, starting transfers between devices, body(): lax.ppermute(held, 'row', [(r, (r + s) % rows) for r in range(rows)])  22.7 us
    pallas_call x13, Pallas kernels, product(): pl.pallas_call(lambda *refs: product_kernel(len(pieces), nx, len(sets), g...  17.6 us
    ppermute x4, waiting for transfers between devices, body(): paired[i][1] = lax.ppermute(done[k], 'layer', pairs[1:3])  17.3 us
    ppermute x10, waiting for transfers between devices, multiply(): lax.ppermute(found[t][k], 'col', along_y(t))  16.7 us
    ppermute x7, waiting for transfers between devices, body(): paired[i] = (lax.ppermute(give, 'layer', pairs),) * 2  14 us
    ppermute x10, starting transfers between devices, multiply(): lax.ppermute(found[t][k], 'col', along_y(t))  12.9 us
  transfers between devices with their start and end apart: 53, of which 18 were waited for; matrix products, arithmetic and copies ran while one was open for 4% of the time, Pallas kernels for 10%

profile of v3, /device:TPU:0, one launch (start us, length us, event | category | flops | bytes accessed | tf_op | source)
XLA Modules:
  0.0 222.4 jit_solution(16788855482964690071)
XLA Ops:
  7.5 12.9 %collective-permute-start.2 = (f32[1024,256]{1,0:T(8,128)S(1)}, f32[1024,256]{1,0:T(8,128)}, u32[]{:S(2)}, u32[]{:S(2)}) collective-permute-start(f32[1024,256]{1,0:T(8,128)S(1)} %broadcast_select_fusion.1.refs_1_), channel_id=1, source_target_pairs={{0,4},{4,0},{1,5},{5,1},{2,6},{6,2},{3,7},{7,3},{8,12},{12,8},{9,1... | collective-permute-start | bytes 3145736 | tf_op jit(solution)/shard_map/ppermute | solution.py:192
  21.7 9.9 %collective-permute-start.4 = (f32[1024,256]{1,0:T(8,128)S(1)}, f32[1024,256]{1,0:T(8,128)}, u32[]{:S(2)}, u32[]{:S(2)}) collective-permute-start(f32[1024,256]{1,0:T(8,128)S(1)} %broadcast_select_fusion.refs_1_), channel_id=1, source_target_pairs={{0,4},{4,0},{1,5},{5,1},{2,6},{6,2},{3,7},{7,3},{8,12},{12,8},{9,1... | collective-permute-start | bytes 3145736 | tf_op jit(solution)/shard_map/ppermute | solution.py:192
  39.2 6.1 %collective-permute-done.6.refs_1_ = f32[192,512]{1,0:T(8,128)S(1)} collective-permute-done((f32[192,512]{1,0:T(8,128)S(1)}, f32[192,512]{1,0:T(8,128)S(1)}, u32[]{:S(2)}, u32[]{:S(2)}) %collective-permute-start.6) | collective-permute-done | bytes 393248 | tf_op jit(solution)/shard_map/ppermute | solution.py:180
  51.3 2.5 %collective-permute-done.14.refs_1_ = f32[192,512]{1,0:T(8,128)} collective-permute-done((f32[192,512]{1,0:T(8,128)}, f32[192,512]{1,0:T(8,128)}, u32[]{:S(2)}, u32[]{:S(2)}) %collective-permute-start.14) | collective-permute-done | bytes 393248 | tf_op jit(solution)/shard_map/ppermute | solution.py:180
  55.4 2.5 %product.18 = (f32[192,512]{1,0:T(8,128)S(1)}, f32[192,512]{1,0:T(8,128)S(1)}) custom-call(f32[192,512]{1,0:T(8,128)} %get-tuple-element.129.refs_0_, f32[192,512]{1,0:T(8,128)} %collective-permute-done.14.refs_1_, bf16[512,256]{1,0:T(8,128)(2,1)S(1)} %get-tuple-element.65.refs_2_, bf16[512,256]{1,0:T(8,128)(2,1)S(1)} %get-tuple-element.66.refs_3_, ...), custom_call_target="tpu_custom_call" | custom-call | flops 1207959552 | bytes 393216 | tf_op jit(solution)/shard_map/product/pallas_call | solution.py:53
  58.0 4.3 %collective-permute-done.21.refs_1_ = f32[192,512]{1,0:T(8,128)} collective-permute-done((f32[192,512]{1,0:T(8,128)}, f32[192,512]{1,0:T(8,128)}, u32[]{:S(2)}, u32[]{:S(2)}) %collective-permute-start.21) | collective-permute-done | bytes 393248 | tf_op jit(solution)/shard_map/ppermute | solution.py:180
  63.9 2.5 %product.20 = (f32[192,512]{1,0:T(8,128)S(1)}, f32[192,512]{1,0:T(8,128)S(1)}) custom-call(f32[192,512]{1,0:T(8,128)} %get-tuple-element.127.refs_0_, f32[192,512]{1,0:T(8,128)} %collective-permute-done.21.refs_1_, bf16[512,256]{1,0:T(8,128)(2,1)S(1)} %get-tuple-element.65.refs_2_, bf16[512,256]{1,0:T(8,128)(2,1)S(1)} %get-tuple-element.66.refs_3_, ...), custom_call_target="tpu_custom_call" | custom-call | flops 1207959552 | bytes 393216 | tf_op jit(solution)/shard_map/product/pallas_call | solution.py:53
  67.8 3.5 %collective-permute-start.9 = (f32[192,512]{1,0:T(8,128)S(1)}, f32[192,512]{1,0:T(8,128)S(1)}, u32[]{:S(2)}, u32[]{:S(2)}) collective-permute-start(f32[192,512]{1,0:T(8,128)S(1)} %combine.26.refs_1_), channel_id=1, source_target_pairs={{0,8},{24,16},{1,9},{25,17},{2,10},{26,18},{3,11},{27,19},{4,12},{... | collective-permute-start | bytes 1179656 | tf_op jit(solution)/shard_map/ppermute | solution.py:226
  71.3 2.9 %collective-permute-done.15.refs_2_ = f32[192,512]{1,0:T(8,128)S(1)} collective-permute-done((f32[192,512]{1,0:T(8,128)S(1)}, f32[192,512]{1,0:T(8,128)S(1)}, u32[]{:S(2)}, u32[]{:S(2)}) %collective-permute-start.15) | collective-permute-done | bytes 393248 | tf_op jit(solution)/shard_map/ppermute | solution.py:208
  76.4 2.6 %collective-permute-done.refs_1_ = f32[192,512]{1,0:T(8,128)S(1)} collective-permute-done((f32[192,512]{1,0:T(8,128)}, f32[192,512]{1,0:T(8,128)S(1)}, u32[]{:S(2)}, u32[]{:S(2)}) %collective-permute-start) | collective-permute-done | bytes 393248 | tf_op jit(solution)/shard_map/ppermute | solution.py:180
  79.0 3.5 %collective-permute-start.16 = (f32[192,512]{1,0:T(8,128)S(1)}, f32[192,512]{1,0:T(8,128)S(1)}, u32[]{:S(2)}, u32[]{:S(2)}) collective-permute-start(f32[192,512]{1,0:T(8,128)S(1)} %combine.29.refs_1_), channel_id=1, source_target_pairs={{0,8},{24,16},{1,9},{25,17},{2,10},{26,18},{3,11},{27,19},{4,12},{... | collective-permute-start | bytes 1179656 | tf_op jit(solution)/shard_map/ppermute | solution.py:226
  89.5 5.4 %collective-permute-done.19.refs_1_ = f32[192,512]{1,0:T(8,128)S(1)} collective-permute-done((f32[192,512]{1,0:T(8,128)S(1)}, f32[192,512]{1,0:T(8,128)S(1)}, u32[]{:S(2)}, u32[]{:S(2)}) %collective-permute-start.19) | collective-permute-done | bytes 393248 | tf_op jit(solution)/shard_map/ppermute | solution.py:180
  96.4 2.1 collective-permute-start.13
  104.7 6.0 %collective-permute-done.48.refs_1_ = f32[128,512]{1,0:T(8,128)S(1)} collective-permute-done((f32[128,512]{1,0:T(8,128)S(1)}, f32[128,512]{1,0:T(8,128)S(1)}, u32[]{:S(2)}, u32[]{:S(2)}) %collective-permute-start.48) | collective-permute-done | bytes 262176 | tf_op jit(solution)/shard_map/ppermute | solution.py:180
  110.7 2.6 %collective-permute-start.20 = (f32[192,512]{1,0:T(8,128)S(1)}, f32[192,512]{1,0:T(8,128)S(1)}, u32[]{:S(2)}, u32[]{:S(2)}) collective-permute-start(f32[192,512]{1,0:T(8,128)S(1)} %get-tuple-element.93), channel_id=1, source_target_pairs={{0,2},{1,3},{2,0},{3,1},{4,6},{5,7},{6,4},{7,5},{8,10},{9,11},{10,... | collective-permute-start | bytes 1179656 | tf_op jit(solution)/shard_map/ppermute | solution.py:208
  113.9 4.4 %collective-permute-start.11 = (f32[192,512]{1,0:T(8,128)S(1)}, f32[192,512]{1,0:T(8,128)S(1)}, u32[]{:S(2)}, u32[]{:S(2)}) collective-permute-start(f32[192,512]{1,0:T(8,128)S(1)} %get-tuple-element.84), channel_id=1, source_target_pairs={{0,8},{8,0},{16,24},{24,16},{1,9},{9,1},{17,25},{25,17},{2,10},{10... | collective-permute-start | bytes 1179656 | tf_op jit(solution)/shard_map/ppermute | solution.py:221
  119.6 10.0 %collective-permute-done.49.refs_2_ = f32[128,512]{1,0:T(8,128)S(1)} collective-permute-done((f32[128,512]{1,0:T(8,128)S(1)}, f32[128,512]{1,0:T(8,128)S(1)}, u32[]{:S(2)}, u32[]{:S(2)}) %collective-permute-start.49) | collective-permute-done | bytes 262176 | tf_op jit(solution)/shard_map/ppermute | solution.py:208
  129.6 2.3 %collective-permute-start.18 = (f32[192,512]{1,0:T(8,128)S(1)}, f32[192,512]{1,0:T(8,128)S(1)}, u32[]{:S(2)}, u32[]{:S(2)}) collective-permute-start(f32[192,512]{1,0:T(8,128)S(1)} %get-tuple-element.90), channel_id=1, source_target_pairs={{0,8},{8,0},{16,24},{24,16},{1,9},{9,1},{17,25},{25,17},{2,10},{10... | collective-permute-start | bytes 1179656 | tf_op jit(solution)/shard_map/ppermute | solution.py:221
  131.9 1.9 collective-permute-start.50
  136.8 7.5 %collective-permute-done.50.refs_2_ = f32[128,512]{1,0:T(8,128)S(1)} collective-permute-done((f32[128,512]{1,0:T(8,128)S(1)}, f32[128,512]{1,0:T(8,128)S(1)}, u32[]{:S(2)}, u32[]{:S(2)}) %collective-permute-start.50) | collective-permute-done | bytes 262176 | tf_op jit(solution)/shard_map/ppermute | solution.py:226
  144.3 2.5 %collective-permute-start.25 = (f32[192,512]{1,0:T(8,128)S(1)}, f32[192,512]{1,0:T(8,128)S(1)}, u32[]{:S(2)}, u32[]{:S(2)}) collective-permute-start(f32[192,512]{1,0:T(8,128)S(1)} %get-tuple-element.96), channel_id=1, source_target_pairs={{0,8},{8,0},{16,24},{24,16},{1,9},{9,1},{17,25},{25,17},{2,10},{10... | collective-permute-start | bytes 1179656 | tf_op jit(solution)/shard_map/ppermute | solution.py:221
  152.1 3.8 %collective-permute-start.29 = (f32[192,512]{1,0:T(8,128)S(1)}, f32[192,512]{1,0:T(8,128)S(1)}, u32[]{:S(2)}, u32[]{:S(2)}) collective-permute-start(f32[192,512]{1,0:T(8,128)S(1)} %get-tuple-element.101), channel_id=1, source_target_pairs={{0,8},{8,0},{16,24},{24,16},{1,9},{9,1},{17,25},{25,17},{2,10},{10... | collective-permute-start | bytes 1179656 | tf_op jit(solution)/shard_map/ppermute | solution.py:221
  162.3 3.8 %collective-permute-start.33 = (f32[192,512]{1,0:T(8,128)S(1)}, f32[192,512]{1,0:T(8,128)S(1)}, u32[]{:S(2)}, u32[]{:S(2)}) collective-permute-start(f32[192,512]{1,0:T(8,128)S(1)} %get-tuple-element.106), channel_id=1, source_target_pairs={{0,8},{8,0},{16,24},{24,16},{1,9},{9,1},{17,25},{25,17},{2,10},{10... | collective-permute-start | bytes 1179656 | tf_op jit(solution)/shard_map/ppermute | solution.py:221
  166.9 3.8 %collective-permute-done.35.refs_2_ = f32[192,512]{1,0:T(8,128)S(1)} collective-permute-done((f32[192,512]{1,0:T(8,128)S(1)}, f32[192,512]{1,0:T(8,128)S(1)}, u32[]{:S(2)}, u32[]{:S(2)}) %collective-permute-start.35) | collective-permute-done | bytes 393248 | tf_op jit(solution)/shard_map/ppermute | solution.py:208
  172.0 2.7 %collective-permute-start.37 = (f32[192,512]{1,0:T(8,128)S(1)}, f32[192,512]{1,0:T(8,128)S(1)}, u32[]{:S(2)}, u32[]{:S(2)}) collective-permute-start(f32[192,512]{1,0:T(8,128)S(1)} %get-tuple-element.111), channel_id=1, source_target_pairs={{0,8},{8,0},{16,24},{24,16},{1,9},{9,1},{17,25},{25,17},{2,10},{10... | collective-permute-start | bytes 1179656 | tf_op jit(solution)/shard_map/ppermute | solution.py:221
  176.3 6.6 %collective-permute-start.41 = (f32[192,512]{1,0:T(8,128)S(1)}, f32[192,512]{1,0:T(8,128)S(1)}, u32[]{:S(2)}, u32[]{:S(2)}) collective-permute-start(f32[192,512]{1,0:T(8,128)S(1)} %get-tuple-element.116), channel_id=1, source_target_pairs={{0,8},{8,0},{16,24},{24,16},{1,9},{9,1},{17,25},{25,17},{2,10},{10... | collective-permute-start | bytes 1179656 | tf_op jit(solution)/shard_map/ppermute | solution.py:221
  183.0 7.1 %collective-permute-done.37.refs_2_ = f32[192,512]{1,0:T(8,128)S(1)} collective-permute-done((f32[192,512]{1,0:T(8,128)S(1)}, f32[192,512]{1,0:T(8,128)S(1)}, u32[]{:S(2)}, u32[]{:S(2)}) %collective-permute-start.37) | collective-permute-done | bytes 393248 | tf_op jit(solution)/shard_map/ppermute | solution.py:221
  192.3 6.3 %collective-permute-done.41.refs_2_ = f32[192,512]{1,0:T(8,128)S(1)} collective-permute-done((f32[192,512]{1,0:T(8,128)S(1)}, f32[192,512]{1,0:T(8,128)S(1)}, u32[]{:S(2)}, u32[]{:S(2)}) %collective-permute-start.41) | collective-permute-done | bytes 393248 | tf_op jit(solution)/shard_map/ppermute | solution.py:221
  202.1 4.8 %collective-permute-done.43 = f32[192,512]{1,0:T(8,128)S(1)} collective-permute-done((f32[192,512]{1,0:T(8,128)S(1)}, f32[192,512]{1,0:T(8,128)S(1)}, u32[]{:S(2)}, u32[]{:S(2)}) %collective-permute-start.43) | collective-permute-done | bytes 393248 | tf_op jit(solution)/shard_map/ppermute | solution.py:229
  207.0 8.3 %collective-permute-done.45 = f32[192,512]{1,0:T(8,128)S(1)} collective-permute-done((f32[192,512]{1,0:T(8,128)S(1)}, f32[192,512]{1,0:T(8,128)S(1)}, u32[]{:S(2)}, u32[]{:S(2)}) %collective-permute-start.45) | collective-permute-done | bytes 393248 | tf_op jit(solution)/shard_map/ppermute | solution.py:229
  215.4 4.2 %collective-permute-done.47 = f32[192,512]{1,0:T(8,128)S(1)} collective-permute-done((f32[192,512]{1,0:T(8,128)S(1)}, f32[192,512]{1,0:T(8,128)S(1)}, u32[]{:S(2)}, u32[]{:S(2)}) %collective-permute-start.47) | collective-permute-done | bytes 393248 | tf_op jit(solution)/shard_map/ppermute | solution.py:229
  219.7 2.0 copy-done.6
  (155 shorter events, 70.5 us)
Async XLA Ops:
  4.3 16.1 %collective-permute-start.3 = (f32[1024,256]{1,0:T(8,128)S(1)}, f32[1024,256]{1,0:T(8,128)}, u32[]{:S(2)}, u32[]{:S(2)}) collective-permute-start(f32[1024,256]{1,0:T(8,128)S(1)} %slice.41), channel_id=1, source_target_pairs={{2,4},{3,5},{4,2},{5,3},{10,12},{11,13},{12,10},{13,11},{18,20},{1... | collective-permute-start | bytes 3145736 | tf_op jit(solution)/shard_map/ppermute | solution.py:175
  7.5 29.4 %collective-permute-start.2 = (f32[1024,256]{1,0:T(8,128)S(1)}, f32[1024,256]{1,0:T(8,128)}, u32[]{:S(2)}, u32[]{:S(2)}) collective-permute-start(f32[1024,256]{1,0:T(8,128)S(1)} %broadcast_select_fusion.1.refs_1_), channel_id=1, source_target_pairs={{0,4},{4,0},{1,5},{5,1},{2,6},{6,2},{3,7},{7,3},{8,12},{12,8},{9,1... | collective-permute-start | bytes 3145736 | tf_op jit(solution)/shard_map/ppermute | solution.py:192
  21.7 25.5 %collective-permute-start.4 = (f32[1024,256]{1,0:T(8,128)S(1)}, f32[1024,256]{1,0:T(8,128)}, u32[]{:S(2)}, u32[]{:S(2)}) collective-permute-start(f32[1024,256]{1,0:T(8,128)S(1)} %broadcast_select_fusion.refs_1_), channel_id=1, source_target_pairs={{0,4},{4,0},{1,5},{5,1},{2,6},{6,2},{3,7},{7,3},{8,12},{12,8},{9,1... | collective-permute-start | bytes 3145736 | tf_op jit(solution)/shard_map/ppermute | solution.py:192
  34.8 19.0 %collective-permute-start.14 = (f32[192,512]{1,0:T(8,128)}, f32[192,512]{1,0:T(8,128)}, u32[]{:S(2)}, u32[]{:S(2)}) collective-permute-start(f32[192,512]{1,0:T(8,128)} %get-tuple-element.129.refs_0_), channel_id=1, source_target_pairs={{0,1},{1,0},{2,3},{3,2},{4,5},{5,4},{6,7},{7,6},{8,9},{9,8},{10,11... | collective-permute-start | bytes 1179656 | tf_op jit(solution)/shard_map/ppermute | solution.py:180
  35.3 26.9 %collective-permute-start.21 = (f32[192,512]{1,0:T(8,128)}, f32[192,512]{1,0:T(8,128)}, u32[]{:S(2)}, u32[]{:S(2)}) collective-permute-start(f32[192,512]{1,0:T(8,128)} %get-tuple-element.127.refs_0_), channel_id=1, source_target_pairs={{0,1},{1,0},{2,3},{3,2},{4,5},{5,4},{6,7},{7,6},{8,9},{9,8},{10,11... | collective-permute-start | bytes 1179656 | tf_op jit(solution)/shard_map/ppermute | solution.py:180
  36.9 38.9 %collective-permute-start.26 = (f32[192,512]{1,0:T(8,128)}, f32[192,512]{1,0:T(8,128)S(1)}, u32[]{:S(2)}, u32[]{:S(2)}) collective-permute-start(f32[192,512]{1,0:T(8,128)} %get-tuple-element.126.refs_0_), channel_id=1, source_target_pairs={{0,1},{1,0},{2,3},{3,2},{4,5},{5,4},{6,7},{7,6},{8,9},{9,8},{10,11... | collective-permute-start | bytes 1179656 | tf_op jit(solution)/shard_map/ppermute | solution.py:180
  45.3 33.7 %collective-permute-start = (f32[192,512]{1,0:T(8,128)}, f32[192,512]{1,0:T(8,128)S(1)}, u32[]{:S(2)}, u32[]{:S(2)}) collective-permute-start(f32[192,512]{1,0:T(8,128)} %get-tuple-element.132.refs_0_), channel_id=1, source_target_pairs={{0,1},{1,0},{2,3},{3,2},{4,5},{5,4},{6,7},{7,6},{8,9},{9,8},{10,11... | collective-permute-start | bytes 1179656 | tf_op jit(solution)/shard_map/ppermute | solution.py:180
  47.3 19.9 %collective-permute-start.7 = (f32[192,256]{1,0:T(8,128)S(1)}, f32[192,256]{1,0:T(8,128)S(1)}, u32[]{:S(2)}, u32[]{:S(2)}) collective-permute-start(f32[192,256]{1,0:T(8,128)S(1)} %product.15), channel_id=1, source_target_pairs={{0,2},{1,3},{2,0},{3,1},{4,6},{5,7},{6,4},{7,5},{8,10},{9,11},{10,... | collective-permute-start | bytes 589832 | tf_op jit(solution)/shard_map/ppermute | solution.py:197
  67.2 16.7 %collective-permute-start.22 = (f32[192,512]{1,0:T(8,128)S(1)}, f32[192,512]{1,0:T(8,128)S(1)}, u32[]{:S(2)}, u32[]{:S(2)}) collective-permute-start(f32[192,512]{1,0:T(8,128)S(1)} %get-tuple-element.95), channel_id=1, source_target_pairs={{0,2},{1,3},{2,0},{3,1},{4,6},{5,7},{6,4},{7,5},{8,10},{9,11},{10,... | collective-permute-start | bytes 1179656 | tf_op jit(solution)/shard_map/ppermute | solution.py:208
  67.8 17.9 %collective-permute-start.9 = (f32[192,512]{1,0:T(8,128)S(1)}, f32[192,512]{1,0:T(8,128)S(1)}, u32[]{:S(2)}, u32[]{:S(2)}) collective-permute-start(f32[192,512]{1,0:T(8,128)S(1)} %combine.26.refs_1_), channel_id=1, source_target_pairs={{0,8},{24,16},{1,9},{25,17},{2,10},{26,18},{3,11},{27,19},{4,12},{... | collective-permute-start | bytes 1179656 | tf_op jit(solution)/shard_map/ppermute | solution.py:226
  75.8 19.1 %collective-permute-start.19 = (f32[192,512]{1,0:T(8,128)S(1)}, f32[192,512]{1,0:T(8,128)S(1)}, u32[]{:S(2)}, u32[]{:S(2)}) collective-permute-start(f32[192,512]{1,0:T(8,128)S(1)} %copy-done.2), channel_id=1, source_target_pairs={{0,1},{1,0},{2,3},{3,2},{4,5},{5,4},{6,7},{7,6},{8,9},{9,8},{10,11... | collective-permute-start | bytes 1179656 | tf_op jit(solution)/shard_map/ppermute | solution.py:180
  79.0 17.4 %collective-permute-start.16 = (f32[192,512]{1,0:T(8,128)S(1)}, f32[192,512]{1,0:T(8,128)S(1)}, u32[]{:S(2)}, u32[]{:S(2)}) collective-permute-start(f32[192,512]{1,0:T(8,128)S(1)} %combine.29.refs_1_), channel_id=1, source_target_pairs={{0,8},{24,16},{1,9},{25,17},{2,10},{26,18},{3,11},{27,19},{4,12},{... | collective-permute-start | bytes 1179656 | tf_op jit(solution)/shard_map/ppermute | solution.py:226
  87.4 16.5 %collective-permute-start.10 = (f32[192,512]{1,0:T(8,128)S(1)}, f32[192,512]{1,0:T(8,128)S(1)}, u32[]{:S(2)}, u32[]{:S(2)}) collective-permute-start(f32[192,512]{1,0:T(8,128)S(1)} %combine.27.refs_3_), channel_id=1, source_target_pairs={{8,16},{16,8},{9,17},{17,9},{10,18},{18,10},{11,19},{19,11},{12,20... | collective-permute-start | bytes 1179656 | tf_op jit(solution)/shard_map/ppermute | solution.py:236
  94.9 18.4 %collective-permute-start.30 = (f32[192,512]{1,0:T(8,128)S(1)}, f32[192,512]{1,0:T(8,128)S(1)}, u32[]{:S(2)}, u32[]{:S(2)}) collective-permute-start(f32[192,512]{1,0:T(8,128)S(1)} %copy-done.1), channel_id=1, source_target_pairs={{0,1},{1,0},{2,3},{3,2},{4,5},{5,4},{6,7},{7,6},{8,9},{9,8},{10,11... | collective-permute-start | bytes 1179656 | tf_op jit(solution)/shard_map/ppermute | solution.py:180
  96.4 17.6 %collective-permute-start.13 = (f32[192,512]{1,0:T(8,128)S(1)}, f32[192,512]{1,0:T(8,128)S(1)}, u32[]{:S(2)}, u32[]{:S(2)}) collective-permute-start(f32[192,512]{1,0:T(8,128)S(1)} %get-tuple-element.87), channel_id=1, source_target_pairs={{0,2},{1,3},{2,0},{3,1},{4,6},{5,7},{6,4},{7,5},{8,10},{9,11},{10,... | collective-permute-start | bytes 1179656 | tf_op jit(solution)/shard_map/ppermute | solution.py:208
  98.5 20.9 %collective-permute-start.17 = (f32[192,512]{1,0:T(8,128)S(1)}, f32[192,512]{1,0:T(8,128)S(1)}, u32[]{:S(2)}, u32[]{:S(2)}) collective-permute-start(f32[192,512]{1,0:T(8,128)S(1)} %combine.30.refs_3_), channel_id=1, source_target_pairs={{8,16},{16,8},{9,17},{17,9},{10,18},{18,10},{11,19},{19,11},{12,20... | collective-permute-start | bytes 1179656 | tf_op jit(solution)/shard_map/ppermute | solution.py:236
  103.9 30.0 %collective-permute-start.27 = (f32[192,512]{1,0:T(8,128)S(1)}, f32[192,512]{1,0:T(8,128)S(1)}, u32[]{:S(2)}, u32[]{:S(2)}) collective-permute-start(f32[192,512]{1,0:T(8,128)S(1)} %get-tuple-element.99), channel_id=1, source_target_pairs={{0,2},{1,3},{2,0},{3,1},{4,6},{5,7},{6,4},{7,5},{8,10},{9,11},{10,... | collective-permute-start | bytes 1179656 | tf_op jit(solution)/shard_map/ppermute | solution.py:208
  110.7 23.9 %collective-permute-start.20 = (f32[192,512]{1,0:T(8,128)S(1)}, f32[192,512]{1,0:T(8,128)S(1)}, u32[]{:S(2)}, u32[]{:S(2)}) collective-permute-start(f32[192,512]{1,0:T(8,128)S(1)} %get-tuple-element.93), channel_id=1, source_target_pairs={{0,2},{1,3},{2,0},{3,1},{4,6},{5,7},{6,4},{7,5},{8,10},{9,11},{10,... | collective-permute-start | bytes 1179656 | tf_op jit(solution)/shard_map/ppermute | solution.py:208
  113.2 22.9 %collective-permute-start.24 = (f32[192,512]{1,0:T(8,128)S(1)}, f32[192,512]{1,0:T(8,128)S(1)}, u32[]{:S(2)}, u32[]{:S(2)}) collective-permute-start(f32[192,512]{1,0:T(8,128)S(1)} %combine.33.refs_3_), channel_id=1, source_target_pairs={{8,16},{16,8},{9,17},{17,9},{10,18},{18,10},{11,19},{19,11},{12,20... | collective-permute-start | bytes 1179656 | tf_op jit(solution)/shard_map/ppermute | solution.py:236
  113.9 18.0 %collective-permute-start.11 = (f32[192,512]{1,0:T(8,128)S(1)}, f32[192,512]{1,0:T(8,128)S(1)}, u32[]{:S(2)}, u32[]{:S(2)}) collective-permute-start(f32[192,512]{1,0:T(8,128)S(1)} %get-tuple-element.84), channel_id=1, source_target_pairs={{0,8},{8,0},{16,24},{24,16},{1,9},{9,1},{17,25},{25,17},{2,10},{10... | collective-permute-start | bytes 1179656 | tf_op jit(solution)/shard_map/ppermute | solution.py:221
  129.6 17.2 %collective-permute-start.18 = (f32[192,512]{1,0:T(8,128)S(1)}, f32[192,512]{1,0:T(8,128)S(1)}, u32[]{:S(2)}, u32[]{:S(2)}) collective-permute-start(f32[192,512]{1,0:T(8,128)S(1)} %get-tuple-element.90), channel_id=1, source_target_pairs={{0,8},{8,0},{16,24},{24,16},{1,9},{9,1},{17,25},{25,17},{2,10},{10... | collective-permute-start | bytes 1179656 | tf_op jit(solution)/shard_map/ppermute | solution.py:221
  133.9 15.0 %collective-permute-start.28 = (f32[192,512]{1,0:T(8,128)S(1)}, f32[192,512]{1,0:T(8,128)S(1)}, u32[]{:S(2)}, u32[]{:S(2)}) collective-permute-start(f32[192,512]{1,0:T(8,128)S(1)} %combine.35.refs_3_), channel_id=1, source_target_pairs={{8,16},{16,8},{9,17},{17,9},{10,18},{18,10},{11,19},{19,11},{12,20... | collective-permute-start | bytes 1179656 | tf_op jit(solution)/shard_map/ppermute | solution.py:236
  134.6 15.9 %collective-permute-start.38 = (f32[192,512]{1,0:T(8,128)S(1)}, f32[192,512]{1,0:T(8,128)S(1)}, u32[]{:S(2)}, u32[]{:S(2)}) collective-permute-start(f32[192,512]{1,0:T(8,128)S(1)} %copy-done), channel_id=1, source_target_pairs={{0,1},{1,0},{2,3},{3,2},{4,5},{5,4},{6,7},{7,6},{8,9},{9,8},{10,11... | collective-permute-start | bytes 1179656 | tf_op jit(solution)/shard_map/ppermute | solution.py:180
  136.2 15.9 %collective-permute-start.34 = (f32[192,512]{1,0:T(8,128)S(1)}, f32[192,512]{1,0:T(8,128)S(1)}, u32[]{:S(2)}, u32[]{:S(2)}) collective-permute-start(f32[192,512]{1,0:T(8,128)S(1)} %get-tuple-element.124.refs_0_), channel_id=1, source_target_pairs={{0,1},{1,0},{2,3},{3,2},{4,5},{5,4},{6,7},{7,6},{8,9},{9,8},{10,11... | collective-permute-start | bytes 1179656 | tf_op jit(solution)/shard_map/ppermute | solution.py:180
  144.3 15.5 %collective-permute-start.25 = (f32[192,512]{1,0:T(8,128)S(1)}, f32[192,512]{1,0:T(8,128)S(1)}, u32[]{:S(2)}, u32[]{:S(2)}) collective-permute-start(f32[192,512]{1,0:T(8,128)S(1)} %get-tuple-element.96), channel_id=1, source_target_pairs={{0,8},{8,0},{16,24},{24,16},{1,9},{9,1},{17,25},{25,17},{2,10},{10... | collective-permute-start | bytes 1179656 | tf_op jit(solution)/shard_map/ppermute | solution.py:221
  170.6 49.0 %collective-permute-start.52 = (f32[128,512]{1,0:T(8,128)S(1)}, f32[128,512]{1,0:T(8,128)S(1)}, u32[]{:S(2)}, u32[]{:S(2)}) collective-permute-start(f32[128,512]{1,0:T(8,128)S(1)} %combine.51), channel_id=1, source_target_pairs={{8,0},{16,24},{9,1},{17,25},{10,2},{18,26},{11,3},{19,27},{12,4},{... | collective-permute-start | bytes 786440 | tf_op jit(solution)/shard_map/ppermute | solution.py:229
  172.0 18.1 %collective-permute-start.37 = (f32[192,512]{1,0:T(8,128)S(1)}, f32[192,512]{1,0:T(8,128)S(1)}, u32[]{:S(2)}, u32[]{:S(2)}) collective-permute-start(f32[192,512]{1,0:T(8,128)S(1)} %get-tuple-element.111), channel_id=1, source_target_pairs={{0,8},{8,0},{16,24},{24,16},{1,9},{9,1},{17,25},{25,17},{2,10},{10... | collective-permute-start | bytes 1179656 | tf_op jit(solution)/shard_map/ppermute | solution.py:221
  175.5 15.5 %collective-permute-start.42 = (f32[192,512]{1,0:T(8,128)S(1)}, f32[192,512]{1,0:T(8,128)S(1)}, u32[]{:S(2)}, u32[]{:S(2)}) collective-permute-start(f32[192,512]{1,0:T(8,128)S(1)} %combine.43.refs_1_), channel_id=1, source_target_pairs={{8,16},{16,8},{9,17},{17,9},{10,18},{18,10},{11,19},{19,11},{12,20... | collective-permute-start | bytes 1179656 | tf_op jit(solution)/shard_map/ppermute | solution.py:236
  176.3 22.3 %collective-permute-start.41 = (f32[192,512]{1,0:T(8,128)S(1)}, f32[192,512]{1,0:T(8,128)S(1)}, u32[]{:S(2)}, u32[]{:S(2)}) collective-permute-start(f32[192,512]{1,0:T(8,128)S(1)} %get-tuple-element.116), channel_id=1, source_target_pairs={{0,8},{8,0},{16,24},{24,16},{1,9},{9,1},{17,25},{25,17},{2,10},{10... | collective-permute-start | bytes 1179656 | tf_op jit(solution)/shard_map/ppermute | solution.py:221
  191.0 16.0 %collective-permute-start.43 = (f32[192,512]{1,0:T(8,128)S(1)}, f32[192,512]{1,0:T(8,128)S(1)}, u32[]{:S(2)}, u32[]{:S(2)}) collective-permute-start(f32[192,512]{1,0:T(8,128)S(1)} %combine.44), channel_id=1, source_target_pairs={{8,0},{16,24},{9,1},{17,25},{10,2},{18,26},{11,3},{19,27},{12,4},{... | collective-permute-start | bytes 1179656 | tf_op jit(solution)/shard_map/ppermute | solution.py:229
  199.4 16.0 %collective-permute-start.45 = (f32[192,512]{1,0:T(8,128)S(1)}, f32[192,512]{1,0:T(8,128)S(1)}, u32[]{:S(2)}, u32[]{:S(2)}) collective-permute-start(f32[192,512]{1,0:T(8,128)S(1)} %combine.46), channel_id=1, source_target_pairs={{8,0},{16,24},{9,1},{17,25},{10,2},{18,26},{11,3},{19,27},{12,4},{... | collective-permute-start | bytes 1179656 | tf_op jit(solution)/shard_map/ppermute | solution.py:229
  200.8 18.7 %collective-permute-start.47 = (f32[192,512]{1,0:T(8,128)S(1)}, f32[192,512]{1,0:T(8,128)S(1)}, u32[]{:S(2)}, u32[]{:S(2)}) collective-permute-start(f32[192,512]{1,0:T(8,128)S(1)} %combine.48), channel_id=1, source_target_pairs={{8,0},{16,24},{9,1},{17,25},{10,2},{18,26},{11,3},{19,27},{12,4},{... | collective-permute-start | bytes 1179656 | tf_op jit(solution)/shard_map/ppermute | solution.py:229
  (31 other events, 383.1 us)
